TPU v7x, 32 devices: a whole 2x2x4 slice. The times are simulated.
32 devices in a mesh: cells: 16 (over z, y, core), genes: 2 (over x).
Axes of the slice: x: 2, y: 2, z: 4, core: 2. Of those that a mesh axis runs over, the one named last changes fastest.
Arguments:
- counts: int32 [2048, 33280], P('cells', 'genes'), may hold values from 0 to 64, as said below
- live_rows: int32 [16], P('cells'), may hold values from 64 to 128, as said below
- left_basis: float32 [32, 2048], P(None, 'cells'), may hold values from -0.125 to 0.125
- right_basis: float32 [32, 33280], P(None, 'genes'), may hold values from -0.03125 to 0.03125
- right_start: float32 [16, 33280], P(None, 'genes'), may hold values from -0.03125 to 0.03125
Outputs:
- left_vectors: float32 [48, 2048], P(None, 'cells')
- right_vectors: float32 [48, 33280], P(None, 'genes')
- diag_blocks: float32 [3, 16, 16], replicated
- couple_blocks: float32 [3, 16, 16], replicated
Inputs may be any that keep to these rules, and one draw needn't show every extreme that they name: `counts`: rows of a cell block at or beyond its live count are padding and are not part of the matrix. `live_rows`: entry b is the number of live rows, the first ones, of cell block b; some block is full in every draw.
All inputs are finite; a program needn't handle non-finite values.
Results may differ from a plain program's by a relative error of at most 0.0003.
Values sent between devices are 32-bit elements; how exact they have to be, the bound alone decides.
A program may use at most 64 MiB of HBM per device.

v0:
```python
import functools
import math

import jax
import jax.numpy as jnp
from jax import lax
from jax.experimental import pallas as pl
from jax.experimental.pallas import tpu as pltpu
from jax.sharding import PartitionSpec as P

BASIS = 32
BLOCK = 16
STEPS = 3
SLOTS = BASIS + STEPS * BLOCK
LANES = 128
F32 = jnp.float32
BF16 = jnp.bfloat16
HIGHEST = lax.Precision.HIGHEST
MESH = pl.DeviceIdType.MESH


def exact(lhs, rhs):
    return jnp.dot(lhs, rhs, precision=HIGHEST, preferred_element_type=F32)


def exact_rows(lhs, rhs):
    return lax.dot_general(
        lhs, rhs, (((1,), (1,)), ((), ())), precision=HIGHEST, preferred_element_type=F32
    )


def split(values):
    high = values.astype(BF16)
    return high, (values - high.astype(F32)).astype(BF16)


def product(high, both, rhs_high, rhs_low, dims):
    rows = high.shape[0]
    first = lax.dot_general(both, rhs_high, (dims, ((), ())), preferred_element_type=F32)
    second = lax.dot_general(high, rhs_low, (dims, ((), ())), preferred_element_type=F32)
    return first[:rows] + (first[rows:] + second)


ALONG = ((1,), (0,))
ROWS = ((1,), (1,))


def loop(start, stop, step):
    def one(k, carry):
        step(k)
        return carry

    lax.fori_loop(start, stop, one, 0)


def orthonormal(gram, near, lower, spanning, vectors):
    lane = lax.broadcasted_iota(jnp.int32, (BLOCK, LANES), 1)
    row = lax.broadcasted_iota(jnp.int32, (BLOCK, LANES), 0)
    coeffs = jnp.where(lane < SLOTS, gram, 0.0)
    squares = gram[:, SLOTS : SLOTS + BLOCK]
    combined = coeffs + coeffs - (exact(coeffs, near) + exact_rows(coeffs, lower))
    residue = coeffs - (exact(combined, near) + exact_rows(combined, lower))
    squares = squares - exact_rows(combined, coeffs) - exact_rows(residue, combined)
    cleaned = vectors - exact(combined, spanning)
    change = jnp.where(lane == row + SLOTS, 1.0, -combined)
    parts = [squares, cleaned, residue, change]
    for k in range(BLOCK):
        pivot = parts[0][k : k + 1, k : k + 1]
        root = lax.rsqrt(pivot)
        root = root * (1.5 - 0.5 * pivot * root * root)
        column = parts[0][:, k : k + 1] * root
        after = []
        for part in parts:
            scaled = part[k : k + 1, :] * root
            places = lax.broadcasted_iota(jnp.int32, part.shape, 0)
            after.append(
                jnp.where(places > k, part - column * scaled, jnp.where(places == k, scaled, part))
            )
        parts = after
    spot = lax.broadcasted_iota(jnp.int32, (BLOCK, BLOCK), 0)
    other = lax.broadcasted_iota(jnp.int32, (BLOCK, BLOCK), 1)
    upper = jnp.where(other >= spot, parts[0], 0.0)
    factor = exact_rows(jnp.where(other == spot, 1.0, 0.0).astype(F32), upper)
    return parts[1], factor, parts[2], parts[3]


def kernel(
    n, g, width, scales,
    live, counts, left_basis, right_basis, right_start,
    left_out, right_out, diag_out, couple_out,
    cnt, logged, bhi, blo, rb, sl, mr, el, tl, er, tr,
    w, ra, rt, rz, pb, w8, ra8, rt8, rz8, pb8, chg, gram0, gram, xg0, xg,
    in_sem, as_sem, ar_sem, bs_sem, br_sem, cs_sem, cr_sem, ds_sem, fs_sem, zs_sem, zr_sem,
    g0s_sem, g0r_sem, gs_sem, gr_sem, x0s_sem, x0r_sem, xs_sem, xr_sem,
):
    cells, genes = counts.shape
    me = lax.axis_index("cells")
    mine = lax.axis_index("genes")
    core = lax.rem(me, 2)
    chip = me // 2
    h = n // 2
    b = 1 << ((h.bit_length() - 1) // 2)
    b = b if h % b == 0 else 1
    a = h // b
    zi, yi = chip // b, lax.rem(chip, b)
    sibling = me + 1 - 2 * core

    def along_cells(src, dst, send, recv, peer):
        return pltpu.make_async_remote_copy(
            src_ref=src, dst_ref=dst, send_sem=send, recv_sem=recv,
            device_id=(peer, mine), device_id_type=MESH,
        )

    def along_genes(src, dst, send, recv, peer):
        return pltpu.make_async_remote_copy(
            src_ref=src, dst_ref=dst, send_sem=send, recv_sem=recv,
            device_id=(me, peer), device_id_type=MESH,
        )

    loads = []
    for d in range(n):
        cols = max(0, min(width, genes - d * width))
        if cols:
            here = pl.ds(d * width, cols)
            loads.append((d, [
                pltpu.make_async_copy(counts.at[:, here], cnt.at[d, :, pl.ds(0, cols)], in_sem.at[d, 0]),
                pltpu.make_async_copy(right_basis.at[:, here], rb.at[d, pl.ds(0, BASIS), pl.ds(0, cols)], in_sem.at[d, 1]),
                pltpu.make_async_copy(right_start.at[:, here], rb.at[d, pl.ds(BASIS, BLOCK), pl.ds(0, cols)], in_sem.at[d, 2]),
            ]))
        if cols < width:
            cnt[d, :, cols:] = jnp.zeros((cells, width - cols), jnp.int32)
            rb[d, :, cols:] = jnp.zeros((BASIS + BLOCK, width - cols), F32)
    for _, trio in loads:
        trio[0].start()
    for _, trio in loads:
        trio[1].start()
        trio[2].start()

    barrier = pltpu.get_barrier_semaphore()

    def greet_cells(k):
        pl.semaphore_signal(barrier, inc=1, device_id=(lax.rem(me + k, n), mine), device_id_type=MESH)

    def greet_genes(k):
        pl.semaphore_signal(barrier, inc=1, device_id=(me, lax.rem(mine + k, g)), device_id_type=MESH)

    loop(1, n, greet_cells)
    loop(1, g, greet_genes)
    pl.semaphore_wait(barrier, n - 1 + g - 1)

    def spread(copy, buf, at, size, send, recv):
        def go(k):
            copy(buf.at[at], buf.at[at], send.at[k], recv.at[at], lax.rem(at + k, size)).start()

        loop(1, size, go)

    def gathered(copy, buf, at, size, send, recv):
        def end(k):
            source = lax.rem(at + size - k, size)
            item = copy(buf.at[source], buf.at[source], send.at[k], recv.at[source], lax.rem(at + k, size))
            item.wait_send()
            item.wait_recv()

        loop(1, size, end)
        return lax.fori_loop(
            1, size, lambda k, total: total + buf[k], buf[0]
        )

    def order(k):
        return lax.rem(zi + 1 + lax.rem(k, a), a), lax.rem(yi + 1 + k // a, b)

    def reduce_scatter(produce, part, fromcore, fromy, fromz, result):
        def first(k):
            z, y = order(k)
            t = z * b + y
            d = 2 * t + 1 - core
            produce(d)
            along_cells(part.at[d], fromcore.at[t], as_sem.at[t], ar_sem.at[t], sibling).start()

        loop(0, h, first)

        def join(t):
            d = 2 * t + core
            produce(d)
            along_cells(part.at[d], fromcore.at[t], as_sem.at[t], ar_sem.at[t], sibling).wait_recv()
            part[d] = part[d] + fromcore[t]
            return d

        def second(k):
            z, y = order(k)
            t = z * b + y
            d = join(t)
            to = z * b + yi
            along_cells(part.at[d], fromy.at[to], bs_sem.at[t], br_sem.at[to], 2 * (zi * b + y) + core).start()

        loop(0, h - a, second)

        def complete(z):
            d = join(z * b + yi)

            def add(k):
                source = z * b + lax.rem(yi + k, b)
                along_cells(part.at[d], fromy.at[source], bs_sem.at[source], br_sem.at[source], sibling).wait_recv()
                part[d] = part[d] + fromy[source]

            loop(1, b, add)
            return d

        def third(k):
            z = lax.rem(zi + k, a)
            d = complete(z)
            along_cells(part.at[d], fromz.at[zi], zs_sem.at[z], zr_sem.at[zi], d).start()

        loop(1, a, third)
        complete(zi)
        result[me] = part[me]

        def fourth(k):
            z = lax.rem(zi + a - k, a)
            along_cells(part.at[me], fromz.at[z], zs_sem.at[z], zr_sem.at[z], sibling).wait_recv()
            result[me] = result[me] + fromz[z]

        loop(1, a, fourth)

    def all_gather(part, fromcore, fromy, fromz, result, consume):
        def relay(z):
            t = z * b + yi
            d = 2 * t + core

            def to_y(k):
                y = lax.rem(yi + k, b)
                along_cells(result.at[d], result.at[d], fs_sem.at[z * b + y], cr_sem.at[d], 2 * (zi * b + y) + core).start()

            loop(1, b, to_y)
            along_cells(result.at[d], result.at[d], ds_sem.at[t], cr_sem.at[d], sibling).start()

        def arrived(d):
            along_cells(result.at[d], result.at[d], ds_sem.at[0], cr_sem.at[d], sibling).wait_recv()

        def go(k):
            z = lax.rem(zi + k, a)
            along_cells(result.at[me], result.at[me], cs_sem.at[z], cr_sem.at[me], 2 * (z * b + yi) + core).start()

        loop(1, a, go)
        relay(zi)
        consume(me)

        def pass_z(k):
            z = lax.rem(zi + a - k, a)
            d = 2 * (z * b + yi) + core
            arrived(d)
            relay(z)

        loop(1, a, pass_z)
        loop(1, a, lambda k: consume(2 * (lax.rem(zi + a - k, a) * b + yi) + core))

        def pass_y(k):
            z = lax.rem(zi + a - lax.rem(k, a), a)
            t = z * b + lax.rem(yi + 1 + k // a, b)
            d = 2 * t + core
            arrived(d)
            along_cells(result.at[d], result.at[d], ds_sem.at[t], cr_sem.at[d], sibling).start()
            consume(d)

        loop(0, h - a, pass_y)

        def rest(k):
            z = lax.rem(zi + a - lax.rem(k, a), a)
            t = z * b + lax.rem(yi + k // a, b)
            d = 2 * t + 1 - core
            arrived(d)
            consume(d)

        loop(0, h, rest)

        def ended(t):
            along_cells(part.at[t], fromcore.at[t], as_sem.at[t], ar_sem.at[t], sibling).wait_send()
            along_cells(result.at[t], result.at[t], ds_sem.at[t], cr_sem.at[t], sibling).wait_send()

        loop(0, h, ended)

        def ended_y(k):
            z, y = order(k)
            t = z * b + y
            along_cells(part.at[t], fromy.at[t], bs_sem.at[t], br_sem.at[t], sibling).wait_send()
            along_cells(result.at[t], result.at[t], fs_sem.at[t], cr_sem.at[t], sibling).wait_send()

        loop(0, h - a, ended_y)

        def ended_z(k):
            z = lax.rem(zi + k, a)
            along_cells(part.at[z], fromz.at[z], zs_sem.at[z], zr_sem.at[z], sibling).wait_send()
            along_cells(result.at[z], result.at[z], cs_sem.at[z], cr_sem.at[z], sibling).wait_send()

        loop(1, a, ended_z)

    live_here = live[0]
    weights_row = jnp.where(
        lax.broadcasted_iota(jnp.int32, (1, cells), 1) < live_here, 1.0, 0.0
    ).astype(F32)
    weights = jnp.where(
        lax.broadcasted_iota(jnp.int32, (cells, LANES), 0) < live_here, 1.0, 0.0
    ).astype(F32)
    for table in (sl, mr, tl, tr):
        table[...] = jnp.zeros_like(table)
    same = jnp.where(
        lax.broadcasted_iota(jnp.int32, (LANES, LANES), 0)
        == lax.broadcasted_iota(jnp.int32, (LANES, LANES), 1),
        1.0, 0.0,
    ).astype(F32)
    el[...] = same
    er[...] = same
    sl[0:BASIS] = left_basis[...] * weights_row
    gram0[me] = exact_rows(sl[0:BASIS], sl[...])
    spread(along_cells, gram0, me, n, g0s_sem, g0r_sem)

    for _, trio in loads:
        trio[0].wait()
    tiles = width // LANES

    def take_log(d):
        for i in range(tiles):
            here = slice(i * LANES, (i + 1) * LANES)
            values = jnp.log(1.0 + cnt[d, :, here].astype(F32)) * weights
            logged[d, :, here] = values
            w8[d, :, here] = jnp.sum(values.reshape(cells // 8, 8, LANES), axis=0)

    loop(0, n, take_log)
    total_at, total_lane = genes // width, genes % width
    w8[total_at, :, total_lane : total_lane + LANES] = jnp.where(
        lax.broadcasted_iota(jnp.int32, (8, LANES), 0) == 0, live_here.astype(F32), 0.0
    )

    reduce_scatter(lambda d: None, w8, ra8, rt8, rz8, pb8)
    for _, trio in loads:
        trio[1].wait()
        trio[2].wait()

    def fill(d):
        high, low = split(rb[d])
        bhi[d, cells : cells + BASIS + BLOCK] = high
        blo[d, cells : cells + BASIS + BLOCK] = low
        blank = jnp.zeros((LANES - BASIS - BLOCK, width), BF16)
        bhi[d, cells + BASIS + BLOCK :] = blank
        blo[d, cells + BASIS + BLOCK :] = blank

    loop(0, n, fill)
    all_gather(w8, ra8, rt8, rz8, pb8, lambda d: None)
    live_total = jnp.sum(
        pb8[total_at, :, total_lane : total_lane + LANES], axis=0, keepdims=True
    )
    inverse = 1.0 / live_total
    factor_scale = lax.rsqrt(live_total)
    factor_scale = factor_scale * (1.5 - 0.5 * live_total * factor_scale * factor_scale)

    xg0[mine] = jnp.zeros((BASIS + BLOCK, 2 * LANES), F32)

    def center(d):
        for i in range(tiles):
            here = slice(i * LANES, (i + 1) * LANES)
            mean = jnp.sum(pb8[d, :, here], axis=0, keepdims=True) * inverse
            mean = jnp.where(d * width + i * LANES < genes, mean, 0.0)
            high, low = split((logged[d, :, here] - weights * mean) * factor_scale)
            bhi[d, 0:cells, here] = high
            blo[d, 0:cells, here] = low
        high, low = split(rb[d])
        both = jnp.concatenate([high, low], axis=0)
        xg0[mine] = xg0[mine] + product(high, both, bhi[d], blo[d], ROWS)

    loop(0, n, center)
    spread(along_genes, xg0, mine, g, x0s_sem, x0r_sem)
    el[0:BASIS] = gathered(along_cells, gram0, me, n, g0s_sem, g0r_sem)
    el[...] = jnp.where((same > 0) & (lax.broadcasted_iota(jnp.int32, (LANES, LANES), 0) >= BASIS), 1.0, el[...])
    cross = gathered(along_genes, xg0, mine, g, x0s_sem, x0r_sem)
    mr[0 : BASIS + BLOCK] = cross[:, :cells]
    er[0 : BASIS + BLOCK] = cross[:, cells:]
    whole = genes // width

    def update(j):
        later = cells + BASIS + (j + 1) * BLOCK
        later = later if isinstance(j, int) else pl.multiple_of(later, BLOCK)
        chigh, clow = split(chg[...])
        cboth = jnp.concatenate([chigh, clow], axis=0)

        def right(d):
            fresh = product(chigh, cboth, bhi[d, cells:], blo[d, cells:], ALONG)
            vhigh, vlow = split(fresh)
            bhi[d, pl.ds(later, BLOCK)] = vhigh
            blo[d, pl.ds(later, BLOCK)] = vlow
            return fresh * scales[1]

        rows = pl.ds(j * BLOCK if isinstance(j, int) else pl.multiple_of(j * BLOCK, BLOCK), BLOCK)

        def emit(d):
            right_out[rows, pl.ds(pl.multiple_of(d * width, LANES), width)] = right(d)

        loop(0, whole, emit)
        if genes % width:
            right_out[rows, whole * width : genes] = right(whole)[:, : genes % width]

    def step(j):
        position = pl.multiple_of(BASIS + j * BLOCK, BLOCK)
        vectors = mr[pl.ds(position, BLOCK)]
        sl[SLOTS : SLOTS + BLOCK] = vectors
        gram[me] = exact_rows(vectors, sl[...])
        spread(along_cells, gram, me, n, gs_sem, gr_sem)
        pl.when(j > 0)(lambda: update(j - 1))
        total = gathered(along_cells, gram, me, n, gs_sem, gr_sem)
        leftvec, factor, against, _ = orthonormal(total, el[...], tl[...], sl[...], vectors)
        diag_out[j] = factor
        sl[pl.ds(position, BLOCK)] = leftvec
        el[pl.ds(position, BLOCK)] = el[pl.ds(position, BLOCK)] + against
        tl[pl.ds(position, BLOCK)] = against
        left_out[pl.ds(position - BASIS, BLOCK)] = leftvec * scales[0]
        high, low = split(leftvec)
        both = jnp.concatenate([high, low], axis=0)

        def produce(d):
            w[d] = product(high, both, bhi[d, 0:cells], blo[d, 0:cells], ALONG)

        reduce_scatter(produce, w, ra, rt, rz, pb)
        xg[j, mine] = jnp.zeros((BLOCK, 2 * LANES), F32)

        def consume(d):
            phigh, plow = split(pb[d])
            bhi[d, cells + SLOTS : cells + SLOTS + BLOCK] = phigh
            blo[d, cells + SLOTS : cells + SLOTS + BLOCK] = plow
            pboth = jnp.concatenate([phigh, plow], axis=0)
            xg[j, mine] = xg[j, mine] + product(phigh, pboth, bhi[d], blo[d], ROWS)

        all_gather(w, ra, rt, rz, pb, consume)
        box = xg.at[j]
        spread(along_genes, box, mine, g, xs_sem.at[j], xr_sem.at[j])
        total = gathered(along_genes, box, mine, g, xs_sem.at[j], xr_sem.at[j])
        projected, factor, against, change = orthonormal(
            total[:, cells:], er[...], tr[...], mr[...], total[:, :cells]
        )
        couple_out[j] = factor
        later = pl.multiple_of(position + BLOCK, BLOCK)
        mr[pl.ds(later, BLOCK)] = projected
        er[pl.ds(later, BLOCK)] = er[pl.ds(later, BLOCK)] + against
        tr[pl.ds(later, BLOCK)] = against
        chg[...] = change

    loop(0, STEPS, step)
    update(STEPS - 1)


def body(counts, live_rows, left_basis, right_basis, right_start):
    cells, genes = counts.shape
    n = lax.axis_size("cells")
    g = lax.axis_size("genes")
    h = n // 2
    width = -(-(genes // LANES + 1) // n) * LANES
    scales = (math.sqrt(float(cells * n)), math.sqrt(float(genes * g)))
    vmem = pl.BlockSpec(memory_space=pltpu.VMEM)
    anywhere = pl.BlockSpec(memory_space=pl.ANY)
    square = pltpu.VMEM((LANES, LANES), F32)
    dma = lambda *shape: pltpu.SemaphoreType.DMA(shape)
    out_shape = (
        jax.ShapeDtypeStruct((STEPS * BLOCK, cells), F32),
        jax.ShapeDtypeStruct((STEPS * BLOCK, genes), F32),
        jax.ShapeDtypeStruct((STEPS, BLOCK, BLOCK), F32),
        jax.ShapeDtypeStruct((STEPS, BLOCK, BLOCK), F32),
    )
    buffers = lambda rows: [
        pltpu.VMEM((n, rows, width), F32),
        pltpu.VMEM((h, rows, width), F32),
        pltpu.VMEM((h, rows, width), F32),
        pltpu.VMEM((h, rows, width), F32),
        pltpu.VMEM((n, rows, width), F32),
    ]
    scratch = [
        pltpu.VMEM((n, cells, width), jnp.int32),
        pltpu.VMEM((n, cells, width), F32),
        pltpu.VMEM((n, cells + LANES, width), BF16),
        pltpu.VMEM((n, cells + LANES, width), BF16),
        pltpu.VMEM((n, BASIS + BLOCK, width), F32),
        square, square, square, square, square, square,
        *buffers(BLOCK),
        *buffers(8),
        pltpu.VMEM((BLOCK, LANES), F32),
        pltpu.VMEM((n, BASIS, LANES), F32),
        pltpu.VMEM((n, BLOCK, LANES), F32),
        pltpu.VMEM((g, BASIS + BLOCK, 2 * LANES), F32),
        pltpu.VMEM((STEPS, g, BLOCK, 2 * LANES), F32),
        dma(n, 3),
        dma(h), dma(h), dma(h), dma(h), dma(h), dma(n), dma(h), dma(h), dma(h), dma(h),
        dma(n), dma(n), dma(n), dma(n),
        dma(g), dma(g), dma(STEPS, g), dma(STEPS, g),
    ]
    return pl.pallas_call(
        functools.partial(kernel, n, g, width, scales),
        out_shape=out_shape,
        in_specs=[pl.BlockSpec(memory_space=pltpu.SMEM), anywhere, vmem, anywhere, anywhere],
        out_specs=(vmem, vmem, vmem, vmem),
        scratch_shapes=scratch,
        compiler_params=pltpu.CompilerParams(
            collective_id=0, has_side_effects=True, vmem_limit_bytes=66 * 1000 * 1000
        ),
    )(live_rows, counts, left_basis, right_basis, right_start)


def solution(mesh):
    in_specs = (
        P("cells", "genes"),
        P("cells"),
        P(None, "cells"),
        P(None, "genes"),
        P(None, "genes"),
    )
    out_specs = (P(None, "cells"), P(None, "genes"), P(), P())
    return jax.shard_map(body, mesh=mesh, in_specs=in_specs, out_specs=out_specs, check_vma=False)
```

profile of v0, /device:TPU:0, one launch (start us, length us, event | category | flops | bytes accessed | tf_op | source)
XLA Modules:
  0.0 181.0 jit_solution(15896511785507735447)
XLA Ops:
  1.3 173.3 %shard_map.84 = (f32[48,128]{1,0:T(8,128)}, f32[48,16640]{1,0:T(8,128)}, f32[3,16,16]{2,1,0:T(8,128)}, f32[3,16,16]{2,1,0:T(8,128)}) custom-call(s32[1]{0:T(128)S(6)} %copy.13.live, s32[128,16640]{1,0:T(8,128)} %counts.1, f32[32,128]{1,0:T(8,128)} %left_basis.1, f32[32,16640]{1,0:T(8,128)} %right_basis.1, f32[16,16640]{1,0:T(8,128)} %right_start.1), custom_call_target="tpu_custom_call" | custom-call | tf_op jit(solution)/shard_map/pallas_call | solution.py:492
  174.6 1.3 copy.14
  176.0 0.0 copy-start.1
  176.0 0.0 copy-start
  176.0 3.8 %copy.15 = f32[48,16640]{1,0:T(8,128)} copy(f32[48,16640]{1,0:T(8,128)} %get-tuple-element.9) | data formatting | bytes 6389760
  179.8 0.0 copy-done.1
  179.8 0.6 copy.16
  180.4 0.0 copy-done
  180.4 0.6 copy.17
Async XLA Ops:
  176.0 3.8 %copy-start.1 = (f32[3,16,16]{2,1,0:T(8,128)S(1)}, f32[3,16,16]{2,1,0:T(8,128)}, u32[]{:S(2)}) copy-start(f32[3,16,16]{2,1,0:T(8,128)} %get-tuple-element.10) | copy-start | bytes 9220
  176.0 4.4 %copy-start = (f32[3,16,16]{2,1,0:T(8,128)S(1)}, f32[3,16,16]{2,1,0:T(8,128)}, u32[]{:S(2)}) copy-start(f32[3,16,16]{2,1,0:T(8,128)} %get-tuple-element.11) | copy-start | bytes 9220
where the time goes:
time: 181 us
  Pallas kernels  173 us (96%)
  local copies, waits for them, and re-layouts  6.37 us (4%)
    pallas_call x1, Pallas kernels, body(): pl.pallas_call(functools.partial(kernel, n, g, width, scales), out_shape=...  173 us
    unnamed x8, local copies, waits for them, and re-layouts  6.37 us

commit v1 on v0

--- a/solution.py
+++ b/solution.py
@@ -12,6 +12,7 @@
 BLOCK = 16
 STEPS = 3
 SLOTS = BASIS + STEPS * BLOCK
+WEIGHT = SLOTS + BLOCK
 LANES = 128
 F32 = jnp.float32
 BF16 = jnp.bfloat16
@@ -89,9 +90,9 @@
     live, counts, left_basis, right_basis, right_start,
     left_out, right_out, diag_out, couple_out,
     cnt, logged, bhi, blo, rb, sl, mr, el, tl, er, tr,
-    w, ra, rt, rz, pb, w8, ra8, rt8, rz8, pb8, chg, gram0, gram, xg0, xg,
+    w, ra, rt, rz, pb, mu, wsum, chg, gram0, gram, xg0, xg,
     in_sem, as_sem, ar_sem, bs_sem, br_sem, cs_sem, cr_sem, ds_sem, fs_sem, zs_sem, zr_sem,
-    g0s_sem, g0r_sem, gs_sem, gr_sem, x0s_sem, x0r_sem, xs_sem, xr_sem,
+    ms_sem, mr_sem, g0s_sem, g0r_sem, gs_sem, gr_sem, x0s_sem, x0r_sem, xs_sem, xr_sem,
 ):
     cells, genes = counts.shape
     me = lax.axis_index("cells")
@@ -146,7 +147,6 @@
 
     loop(1, n, greet_cells)
     loop(1, g, greet_genes)
-    pl.semaphore_wait(barrier, n - 1 + g - 1)
 
     def spread(copy, buf, at, size, send, recv):
         def go(k):
@@ -154,7 +154,7 @@
 
         loop(1, size, go)
 
-    def gathered(copy, buf, at, size, send, recv):
+    def waited(copy, buf, at, size, send, recv):
         def end(k):
             source = lax.rem(at + size - k, size)
             item = copy(buf.at[source], buf.at[source], send.at[k], recv.at[source], lax.rem(at + k, size))
@@ -162,6 +162,9 @@
             item.wait_recv()
 
         loop(1, size, end)
+
+    def gathered(copy, buf, at, size, send, recv):
+        waited(copy, buf, at, size, send, recv)
         return lax.fori_loop(
             1, size, lambda k, total: total + buf[k], buf[0]
         )
@@ -311,30 +314,34 @@
     el[...] = same
     er[...] = same
     sl[0:BASIS] = left_basis[...] * weights_row
-    gram0[me] = exact_rows(sl[0:BASIS], sl[...])
-    spread(along_cells, gram0, me, n, g0s_sem, g0r_sem)
-
-    for _, trio in loads:
-        trio[0].wait()
+    sl[WEIGHT : WEIGHT + 8] = jnp.where(
+        lax.broadcasted_iota(jnp.int32, (8, cells), 0) == 0, weights_row, 0.0
+    )
     tiles = width // LANES
 
     def take_log(d):
         for i in range(tiles):
             here = slice(i * LANES, (i + 1) * LANES)
-            values = jnp.log(1.0 + cnt[d, :, here].astype(F32)) * weights
-            logged[d, :, here] = values
-            w8[d, :, here] = jnp.sum(values.reshape(cells // 8, 8, LANES), axis=0)
-
-    loop(0, n, take_log)
-    total_at, total_lane = genes // width, genes % width
-    w8[total_at, :, total_lane : total_lane + LANES] = jnp.where(
-        lax.broadcasted_iota(jnp.int32, (8, LANES), 0) == 0, live_here.astype(F32), 0.0
-    )
-
-    reduce_scatter(lambda d: None, w8, ra8, rt8, rz8, pb8)
+            logged[d, :, here] = jnp.log(1.0 + cnt[d, :, here].astype(F32)) * weights
+
+    for _, trio in loads:
+        trio[0].wait()
+    take_log(me)
+    portion = 1.0 / jnp.maximum(live_here, 1).astype(F32)
+    for i in range(tiles):
+        here = slice(i * LANES, (i + 1) * LANES)
+        mu[me, :, here] = jnp.sum(logged[me, :, here], axis=0, keepdims=True) * portion
+    gram0[me, 0:BASIS] = exact_rows(sl[0:BASIS], sl[...])
+    gram0[me, BASIS:] = exact_rows(sl[WEIGHT : WEIGHT + 8], sl[...])
+    pl.semaphore_wait(barrier, n - 1 + g - 1)
+    spread(along_cells, mu, me, n, ms_sem, mr_sem)
+    spread(along_cells, gram0, me, n, g0s_sem, g0r_sem)
+    loop(1, n, lambda k: take_log(lax.rem(me + k, n)))
+
     for _, trio in loads:
         trio[1].wait()
         trio[2].wait()
+    xg0[mine] = jnp.zeros((BASIS + BLOCK, 2 * LANES), F32)
 
     def fill(d):
         high, low = split(rb[d])
@@ -343,38 +350,43 @@
         blank = jnp.zeros((LANES - BASIS - BLOCK, width), BF16)
         bhi[d, cells + BASIS + BLOCK :] = blank
         blo[d, cells + BASIS + BLOCK :] = blank
+        both = jnp.concatenate([high, low], axis=0)
+        xg0[mine, :, cells:] = xg0[mine, :, cells:] + product(high, both, bhi[d, cells:], blo[d, cells:], ROWS)
 
     loop(0, n, fill)
-    all_gather(w8, ra8, rt8, rz8, pb8, lambda d: None)
-    live_total = jnp.sum(
-        pb8[total_at, :, total_lane : total_lane + LANES], axis=0, keepdims=True
-    )
+    waited(along_cells, mu, me, n, ms_sem, mr_sem)
+
+    def center(d):
+        for i in range(tiles):
+            here = slice(i * LANES, (i + 1) * LANES)
+            high, low = split(logged[d, :, here] - weights * mu[d, :, here])
+            bhi[d, 0:cells, here] = high
+            blo[d, 0:cells, here] = low
+        high = bhi[d, cells : cells + BASIS + BLOCK]
+        both = jnp.concatenate([high, blo[d, cells : cells + BASIS + BLOCK]], axis=0)
+        xg0[mine, :, :cells] = xg0[mine, :, :cells] + product(high, both, bhi[d, 0:cells], blo[d, 0:cells], ROWS)
+
+    loop(0, n, center)
+    spread(along_genes, xg0, mine, g, x0s_sem, x0r_sem)
+    near = gathered(along_cells, gram0, me, n, g0s_sem, g0r_sem)
+    corner = lax.broadcasted_iota(jnp.int32, (LANES, LANES), 0)
+    across = lax.broadcasted_iota(jnp.int32, (BASIS, LANES), 1)
+    el[...] = jnp.where((same > 0) & (corner >= BASIS), 1.0, 0.0)
+    el[0:BASIS] = jnp.where(across < SLOTS, near[0:BASIS], 0.0)
+    wsum[...] = near[BASIS:]
+    live_total = near[BASIS : BASIS + 1, WEIGHT : WEIGHT + 1]
     inverse = 1.0 / live_total
     factor_scale = lax.rsqrt(live_total)
     factor_scale = factor_scale * (1.5 - 0.5 * live_total * factor_scale * factor_scale)
-
-    xg0[mine] = jnp.zeros((BASIS + BLOCK, 2 * LANES), F32)
-
-    def center(d):
-        for i in range(tiles):
-            here = slice(i * LANES, (i + 1) * LANES)
-            mean = jnp.sum(pb8[d, :, here], axis=0, keepdims=True) * inverse
-            mean = jnp.where(d * width + i * LANES < genes, mean, 0.0)
-            high, low = split((logged[d, :, here] - weights * mean) * factor_scale)
-            bhi[d, 0:cells, here] = high
-            blo[d, 0:cells, here] = low
-        high, low = split(rb[d])
-        both = jnp.concatenate([high, low], axis=0)
-        xg0[mine] = xg0[mine] + product(high, both, bhi[d], blo[d], ROWS)
-
-    loop(0, n, center)
-    spread(along_genes, xg0, mine, g, x0s_sem, x0r_sem)
-    el[0:BASIS] = gathered(along_cells, gram0, me, n, g0s_sem, g0r_sem)
-    el[...] = jnp.where((same > 0) & (lax.broadcasted_iota(jnp.int32, (LANES, LANES), 0) >= BASIS), 1.0, el[...])
     cross = gathered(along_genes, xg0, mine, g, x0s_sem, x0r_sem)
     mr[0 : BASIS + BLOCK] = cross[:, :cells]
     er[0 : BASIS + BLOCK] = cross[:, cells:]
     whole = genes // width
+    lane = lax.broadcasted_iota(jnp.int32, (BLOCK, LANES), 1)
+    row = lax.broadcasted_iota(jnp.int32, (BLOCK, LANES), 0)
+
+    def turned(column, start):
+        return jnp.sum(jnp.where(lane == row + start, column, 0.0), axis=0, keepdims=True)
 
     def update(j):
         later = cells + BASIS + (j + 1) * BLOCK
@@ -406,13 +418,21 @@
         spread(along_cells, gram, me, n, gs_sem, gr_sem)
         pl.when(j > 0)(lambda: update(j - 1))
         total = gathered(along_cells, gram, me, n, gs_sem, gr_sem)
-        leftvec, factor, against, _ = orthonormal(total, el[...], tl[...], sl[...], vectors)
+        held = total[:, WEIGHT : WEIGHT + 1] * inverse
+        weighed = wsum[0:1] + turned(total[:, WEIGHT : WEIGHT + 1], SLOTS)
+        scale = jnp.where(lane < SLOTS, factor_scale, factor_scale * factor_scale)
+        leftvec, factor, against, change = orthonormal(
+            (total - held * weighed) * scale, el[...], tl[...], sl[...],
+            (vectors - held * weights_row) * factor_scale,
+        )
         diag_out[j] = factor
+        tilt = jnp.sum(jnp.where(lane < SLOTS, change * wsum[0:1], 0.0), axis=1, keepdims=True)
+        wsum[0:1] = wsum[0:1] + turned(tilt, position)
         sl[pl.ds(position, BLOCK)] = leftvec
         el[pl.ds(position, BLOCK)] = el[pl.ds(position, BLOCK)] + against
         tl[pl.ds(position, BLOCK)] = against
         left_out[pl.ds(position - BASIS, BLOCK)] = leftvec * scales[0]
-        high, low = split(leftvec)
+        high, low = split((leftvec - tilt * inverse * weights_row) * factor_scale)
         both = jnp.concatenate([high, low], axis=0)
 
         def produce(d):
@@ -451,7 +471,7 @@
     n = lax.axis_size("cells")
     g = lax.axis_size("genes")
     h = n // 2
-    width = -(-(genes // LANES + 1) // n) * LANES
+    width = -(-(genes // LANES) // n) * LANES
     scales = (math.sqrt(float(cells * n)), math.sqrt(float(genes * g)))
     vmem = pl.BlockSpec(memory_space=pltpu.VMEM)
     anywhere = pl.BlockSpec(memory_space=pl.ANY)
@@ -478,15 +498,16 @@
         pltpu.VMEM((n, BASIS + BLOCK, width), F32),
         square, square, square, square, square, square,
         *buffers(BLOCK),
-        *buffers(8),
+        pltpu.VMEM((n, 1, width), F32),
+        pltpu.VMEM((8, LANES), F32),
         pltpu.VMEM((BLOCK, LANES), F32),
-        pltpu.VMEM((n, BASIS, LANES), F32),
+        pltpu.VMEM((n, BASIS + 8, LANES), F32),
         pltpu.VMEM((n, BLOCK, LANES), F32),
         pltpu.VMEM((g, BASIS + BLOCK, 2 * LANES), F32),
         pltpu.VMEM((STEPS, g, BLOCK, 2 * LANES), F32),
         dma(n, 3),
         dma(h), dma(h), dma(h), dma(h), dma(h), dma(n), dma(h), dma(h), dma(h), dma(h),
-        dma(n), dma(n), dma(n), dma(n),
+        dma(n), dma(n), dma(n), dma(n), dma(n), dma(n),
         dma(g), dma(g), dma(STEPS, g), dma(STEPS, g),
     ]
     return pl.pallas_call(

time: 181 us -> 165 us (0.912)
  Pallas kernels: 173 us -> 157 us
    pallas_call x1, Pallas kernels: 173 us -> 157 us  [body(): pl.pallas_call(functools.partial(kernel, n, g, width, scales), out_shape=...]
where the time goes in v1:
time: 165 us
  Pallas kernels  157 us (95%)
  local copies, waits for them, and re-layouts  6.37 us (4%)
    pallas_call x1, Pallas kernels, body(): pl.pallas_call(functools.partial(kernel, n, g, width, scales), out_shape=...  157 us
    unnamed x8, local copies, waits for them, and re-layouts  6.37 us

profile of v1, /device:TPU:0, one launch (start us, length us, event | category | flops | bytes accessed | tf_op | source)
XLA Modules:
  0.0 164.5 jit_solution(8249699513394944341)
XLA Ops:
  1.3 156.9 %shard_map.84 = (f32[48,128]{1,0:T(8,128)}, f32[48,16640]{1,0:T(8,128)}, f32[3,16,16]{2,1,0:T(8,128)}, f32[3,16,16]{2,1,0:T(8,128)}) custom-call(s32[1]{0:T(128)S(6)} %copy.13.live, s32[128,16640]{1,0:T(8,128)} %counts.1, f32[32,128]{1,0:T(8,128)} %left_basis.1, f32[32,16640]{1,0:T(8,128)} %right_basis.1, f32[16,16640]{1,0:T(8,128)} %right_start.1), custom_call_target="tpu_custom_call" | custom-call | tf_op jit(solution)/shard_map/pallas_call | solution.py:513
  158.1 1.3 copy.14
  159.5 0.0 copy-start.1
  159.5 0.0 copy-start
  159.5 3.8 %copy.15 = f32[48,16640]{1,0:T(8,128)} copy(f32[48,16640]{1,0:T(8,128)} %get-tuple-element.9) | data formatting | bytes 6389760
  163.3 0.0 copy-done.1
  163.3 0.6 copy.16
  163.9 0.0 copy-done
  163.9 0.6 copy.17
Async XLA Ops:
  159.5 3.8 %copy-start.1 = (f32[3,16,16]{2,1,0:T(8,128)S(1)}, f32[3,16,16]{2,1,0:T(8,128)}, u32[]{:S(2)}) copy-start(f32[3,16,16]{2,1,0:T(8,128)} %get-tuple-element.10) | copy-start | bytes 9220
  159.5 4.4 %copy-start = (f32[3,16,16]{2,1,0:T(8,128)S(1)}, f32[3,16,16]{2,1,0:T(8,128)}, u32[]{:S(2)}) copy-start(f32[3,16,16]{2,1,0:T(8,128)} %get-tuple-element.11) | copy-start | bytes 9220

commit v2 on v1

v2 whole, which is shorter than its diff:
```python
import functools
import math

import jax
import jax.numpy as jnp
from jax import lax
from jax.experimental import pallas as pl
from jax.experimental.pallas import tpu as pltpu
from jax.sharding import PartitionSpec as P

BASIS = 32
BLOCK = 16
STEPS = 3
SLOTS = BASIS + STEPS * BLOCK
WEIGHT = SLOTS + BLOCK
LANES = 128
F32 = jnp.float32
BF16 = jnp.bfloat16
HIGHEST = lax.Precision.HIGHEST
MESH = pl.DeviceIdType.MESH


def exact(lhs, rhs):
    return jnp.dot(lhs, rhs, precision=HIGHEST, preferred_element_type=F32)


def exact_rows(lhs, rhs):
    return lax.dot_general(
        lhs, rhs, (((1,), (1,)), ((), ())), precision=HIGHEST, preferred_element_type=F32
    )


def split(values):
    high = values.astype(BF16)
    return high, (values - high.astype(F32)).astype(BF16)


def product(high, both, rhs_high, rhs_low, dims):
    rows = high.shape[0]
    first = lax.dot_general(both, rhs_high, (dims, ((), ())), preferred_element_type=F32)
    second = lax.dot_general(high, rhs_low, (dims, ((), ())), preferred_element_type=F32)
    return first[:rows] + (first[rows:] + second)


ALONG = ((1,), (0,))
ROWS = ((1,), (1,))


def loop(start, stop, step):
    def one(k, carry):
        step(k)
        return carry

    lax.fori_loop(start, stop, one, 0)


def orthonormal(gram, near, lower):
    lane = lax.broadcasted_iota(jnp.int32, (BLOCK, LANES), 1)
    row = lax.broadcasted_iota(jnp.int32, (BLOCK, LANES), 0)
    coeffs = jnp.where(lane < SLOTS, gram, 0.0)
    squares = gram[:, SLOTS : SLOTS + BLOCK]
    combined = coeffs + coeffs - (exact(coeffs, near) + exact_rows(coeffs, lower))
    residue = coeffs - (exact(combined, near) + exact_rows(combined, lower))
    squares = squares - exact_rows(combined, coeffs) - exact_rows(residue, combined)
    change = jnp.where(lane == row + SLOTS, 1.0, -combined)
    parts = [squares, residue, change]
    for k in range(BLOCK):
        pivot = parts[0][k : k + 1, k : k + 1]
        root = lax.rsqrt(pivot)
        root = root * (1.5 - 0.5 * pivot * root * root)
        column = parts[0][:, k : k + 1] * root
        after = []
        for part in parts:
            scaled = part[k : k + 1, :] * root
            places = lax.broadcasted_iota(jnp.int32, part.shape, 0)
            after.append(
                jnp.where(places > k, part - column * scaled, jnp.where(places == k, scaled, part))
            )
        parts = after
    spot = lax.broadcasted_iota(jnp.int32, (BLOCK, BLOCK), 0)
    other = lax.broadcasted_iota(jnp.int32, (BLOCK, BLOCK), 1)
    upper = jnp.where(other >= spot, parts[0], 0.0)
    factor = exact_rows(jnp.where(other == spot, 1.0, 0.0).astype(F32), upper)
    return factor, parts[1], parts[2]


def kernel(
    n, g, width, scales,
    live, counts, left_basis, right_basis, right_start,
    left_out, right_out, diag_out, couple_out,
    cnt, logged, bhi, blo, rb, sl, mr, el, tl, er, tr,
    w, ra, rt, rz, wb, rab, rtb, rzb, pb, stack, ground, tpart, tfrom,
    mu, wsum, chg, gram0, gram, xs0, xb0, xg, gx, gy, gz,
    in_sem, as_sem, ar_sem, bs_sem, br_sem, zs_sem, zr_sem,
    bas_sem, bar_sem, bbs_sem, bbr_sem, bzs_sem, bzr_sem,
    cs_sem, cr_sem, ds_sem, fs_sem, ts_sem, tr_sem,
    ms_sem, mr_sem, g0s_sem, g0r_sem, gs_sem, gr_sem, s0s_sem, s0r_sem, b0s_sem, b0r_sem,
    xs_sem, xr_sem, gxs_sem, gxr_sem, gys_sem, gyr_sem, gzs_sem, gzr_sem,
):
    cells, genes = counts.shape
    me = lax.axis_index("cells")
    mine = lax.axis_index("genes")
    core = lax.rem(me, 2)
    chip = me // 2
    h = n // 2
    b = 1 << ((h.bit_length() - 1) // 2)
    b = b if h % b == 0 else 1
    a = h // b
    zi, yi = chip // b, lax.rem(chip, b)
    sibling = me + 1 - 2 * core
    tiles = width // LANES
    whole, spare = genes // width, genes % width
    lane = lax.broadcasted_iota(jnp.int32, (BLOCK, LANES), 1)
    row = lax.broadcasted_iota(jnp.int32, (BLOCK, LANES), 0)

    def along_cells(src, dst, send, recv, peer):
        return pltpu.make_async_remote_copy(
            src_ref=src, dst_ref=dst, send_sem=send, recv_sem=recv,
            device_id=(peer, mine), device_id_type=MESH,
        )

    def along_genes(src, dst, send, recv, peer):
        return pltpu.make_async_remote_copy(
            src_ref=src, dst_ref=dst, send_sem=send, recv_sem=recv,
            device_id=(me, peer), device_id_type=MESH,
        )

    def along_plane(src, dst, send, recv, peer):
        return along_cells(src, dst, send, recv, 2 * b * zi + peer)

    def along_column(src, dst, send, recv, peer):
        return along_cells(src, dst, send, recv, 2 * (peer * b + yi) + core)

    loads = []
    for d in range(n):
        cols = max(0, min(width, genes - d * width))
        if cols:
            here = pl.ds(d * width, cols)
            loads.append((d, [
                pltpu.make_async_copy(counts.at[:, here], cnt.at[d, :, pl.ds(0, cols)], in_sem.at[d, 0]),
                pltpu.make_async_copy(right_basis.at[:, here], rb.at[d, pl.ds(0, BASIS), pl.ds(0, cols)], in_sem.at[d, 1]),
                pltpu.make_async_copy(right_start.at[:, here], rb.at[d, pl.ds(BASIS, BLOCK), pl.ds(0, cols)], in_sem.at[d, 2]),
            ]))
        if cols < width:
            cnt[d, :, cols:] = jnp.zeros((cells, width - cols), jnp.int32)
            rb[d, :, cols:] = jnp.zeros((BASIS + BLOCK, width - cols), F32)
    for _, trio in loads:
        trio[0].start()
    for _, trio in loads:
        trio[1].start()
        trio[2].start()

    barrier = pltpu.get_barrier_semaphore()

    def greet_cells(k):
        pl.semaphore_signal(barrier, inc=1, device_id=(lax.rem(me + k, n), mine), device_id_type=MESH)

    def greet_genes(k):
        pl.semaphore_signal(barrier, inc=1, device_id=(me, lax.rem(mine + k, g)), device_id_type=MESH)

    loop(1, n, greet_cells)
    loop(1, g, greet_genes)

    def spread(copy, buf, at, size, send, recv):
        def go(k):
            copy(buf.at[at], buf.at[at], send.at[k], recv.at[at], lax.rem(at + k, size)).start()

        loop(1, size, go)

    def waited(copy, buf, at, size, send, recv):
        def end(k):
            source = lax.rem(at + size - k, size)
            item = copy(buf.at[source], buf.at[source], send.at[k], recv.at[source], lax.rem(at + k, size))
            item.wait_send()
            item.wait_recv()

        loop(1, size, end)

    def gathered(copy, buf, at, size, send, recv):
        waited(copy, buf, at, size, send, recv)
        return lax.fori_loop(
            1, size, lambda k, total: total + buf[k], buf[0]
        )

    def order(k):
        return lax.rem(zi + 1 + lax.rem(k, a), a), lax.rem(yi + 1 + k // a, b)

    class Scatter:
        def __init__(self, part, fromcore, fromy, fromz, sems):
            self.part, self.fromcore, self.fromy, self.fromz = part, fromcore, fromy, fromz
            self.cs, self.cr, self.ys, self.yr, self.zs, self.zr = sems

        def over(self, d, t):
            return along_cells(self.part.at[d], self.fromcore.at[t], self.cs.at[t], self.cr.at[t], sibling)

        def first(self, produce):
            def one(k):
                z, y = order(k)
                t = z * b + y
                d = 2 * t + 1 - core
                produce(d)
                self.over(d, t).start()

            loop(0, h, one)

        def second(self, produce):
            def one(k, send):
                z, y = order(k)
                t = z * b + y
                d = 2 * t + core
                produce(d)
                self.over(d, t).wait_recv()
                self.part[d] = self.part[d] + self.fromcore[t]
                if send:
                    to = z * b + yi
                    along_cells(
                        self.part.at[d], self.fromy.at[to], self.ys.at[t], self.yr.at[to],
                        2 * (zi * b + y) + core,
                    ).start()

            loop(0, h - a, lambda k: one(k, True))
            loop(h - a, h, lambda k: one(k, False))

        def complete(self, z):
            d = 2 * (z * b + yi) + core

            def add(k):
                source = z * b + lax.rem(yi + k, b)
                along_cells(self.part.at[d], self.fromy.at[source], self.ys.at[source], self.yr.at[source], sibling).wait_recv()
                self.part[d] = self.part[d] + self.fromy[source]

            loop(1, b, add)
            return d

        def third(self):
            def one(k):
                z = lax.rem(zi + k, a)
                d = self.complete(z)
                along_cells(self.part.at[d], self.fromz.at[zi], self.zs.at[z], self.zr.at[zi], d).start()

            loop(1, a, one)
            self.complete(zi)

        def fourth(self, result, rows):
            result[rows] = self.part[me]

            def one(k):
                z = lax.rem(zi + a - k, a)
                along_cells(self.part.at[me], self.fromz.at[z], self.zs.at[z], self.zr.at[z], sibling).wait_recv()
                result[rows] = result[rows] + self.fromz[z]

            loop(1, a, one)

        def ended(self):
            loop(0, h, lambda t: self.over(t, t).wait_send())

            def sent_y(k):
                z, y = order(k)
                t = z * b + y
                along_cells(self.part.at[t], self.fromy.at[t], self.ys.at[t], self.yr.at[t], sibling).wait_send()

            loop(0, h - a, sent_y)

            def sent_z(k):
                z = lax.rem(zi + k, a)
                along_cells(self.part.at[z], self.fromz.at[z], self.zs.at[z], self.zr.at[z], sibling).wait_send()

            loop(1, a, sent_z)

    walk = Scatter(w, ra, rt, rz, (as_sem, ar_sem, bs_sem, br_sem, zs_sem, zr_sem))
    base = Scatter(wb, rab, rtb, rzb, (bas_sem, bar_sem, bbs_sem, bbr_sem, bzs_sem, bzr_sem))

    live_here = live[0]
    weights_row = jnp.where(
        lax.broadcasted_iota(jnp.int32, (1, cells), 1) < live_here, 1.0, 0.0
    ).astype(F32)
    weights = jnp.where(
        lax.broadcasted_iota(jnp.int32, (cells, LANES), 0) < live_here, 1.0, 0.0
    ).astype(F32)
    for table in (sl, mr, tl, tr, stack):
        table[...] = jnp.zeros_like(table)
    same = jnp.where(
        lax.broadcasted_iota(jnp.int32, (LANES, LANES), 0)
        == lax.broadcasted_iota(jnp.int32, (LANES, LANES), 1),
        1.0, 0.0,
    ).astype(F32)
    er[...] = same
    chg[...] = jnp.where(lane == row + SLOTS, 1.0, 0.0)
    sl[0:BASIS] = left_basis[...] * weights_row
    sl[WEIGHT : WEIGHT + 8] = jnp.where(
        lax.broadcasted_iota(jnp.int32, (8, cells), 0) == 0, weights_row, 0.0
    )
    gram0[me, 0:BASIS] = exact_rows(sl[0:BASIS], sl[...])
    gram0[me, BASIS:] = exact_rows(sl[WEIGHT : WEIGHT + 8], sl[...])

    def take_log(d):
        for i in range(tiles):
            here = slice(i * LANES, (i + 1) * LANES)
            logged[d, :, here] = jnp.log(1.0 + cnt[d, :, here].astype(F32)) * weights

    for _, trio in loads:
        trio[0].wait()
    take_log(me)
    portion = 1.0 / jnp.maximum(live_here, 1).astype(F32)
    for i in range(tiles):
        here = slice(i * LANES, (i + 1) * LANES)
        mu[me, :, here] = jnp.sum(logged[me, :, here], axis=0, keepdims=True) * portion
    pl.semaphore_wait(barrier, n - 1 + g - 1)
    spread(along_cells, mu, me, n, ms_sem, mr_sem)
    spread(along_cells, gram0, me, n, g0s_sem, g0r_sem)
    loop(1, n, lambda k: take_log(lax.rem(me + k, n)))

    for _, trio in loads:
        trio[1].wait()
        trio[2].wait()
    xs0[mine] = jnp.zeros((BASIS + BLOCK, LANES), F32)
    xb0[mine] = jnp.zeros((BASIS, LANES), F32)
    xg[0, mine] = jnp.zeros((BLOCK, LANES), F32)

    def fill(d):
        high, low = split(rb[d])
        bhi[d, cells : cells + BASIS + BLOCK] = high
        blo[d, cells : cells + BASIS + BLOCK] = low
        blank = jnp.zeros((LANES - BASIS - BLOCK, width), BF16)
        bhi[d, cells + BASIS + BLOCK :] = blank
        blo[d, cells + BASIS + BLOCK :] = blank
        both = jnp.concatenate([high, low], axis=0)
        xs0[mine] = xs0[mine] + product(high, both, bhi[d, cells:], blo[d, cells:], ROWS)

    loop(0, n, fill)
    spread(along_genes, xs0, mine, g, s0s_sem, s0r_sem)
    waited(along_cells, mu, me, n, ms_sem, mr_sem)

    bhigh, blow = split(jnp.concatenate(
        [sl[0:BASIS], sl[WEIGHT : WEIGHT + 8], jnp.zeros((8, cells), F32)], axis=0
    ))
    bboth = jnp.concatenate([bhigh, blow], axis=0)

    def center(d):
        for i in range(tiles):
            here = slice(i * LANES, (i + 1) * LANES)
            high, low = split(logged[d, :, here] - weights * mu[d, :, here])
            bhi[d, 0:cells, here] = high
            blo[d, 0:cells, here] = low
        high = bhi[d, cells : cells + BASIS + BLOCK]
        both = jnp.concatenate([high, blo[d, cells : cells + BASIS + BLOCK]], axis=0)
        met = product(high, both, bhi[d, 0:cells], blo[d, 0:cells], ROWS)
        xb0[mine] = xb0[mine] + met[0:BASIS]
        xg[0, mine] = xg[0, mine] + met[BASIS:]
        made = product(bhigh, bboth, bhi[d, 0:cells], blo[d, 0:cells], ALONG)
        wb[d] = made[0:BASIS]
        tpart[d] = made[BASIS : BASIS + 1]

    base.first(center)
    base.second(center)
    spread(along_genes, xg.at[0], mine, g, xs_sem.at[0], xr_sem.at[0])
    spread(along_genes, xb0, mine, g, b0s_sem, b0r_sem)

    def give(k):
        d = lax.rem(me + k, n)
        along_cells(tpart.at[d], tfrom.at[me], ts_sem.at[k], tr_sem.at[me], d).start()

    loop(1, n, give)
    near = gathered(along_cells, gram0, me, n, g0s_sem, g0r_sem)
    corner = lax.broadcasted_iota(jnp.int32, (LANES, LANES), 0)
    across = lax.broadcasted_iota(jnp.int32, (BASIS, LANES), 1)
    el[...] = jnp.where((same > 0) & (corner >= BASIS), 1.0, 0.0)
    el[0:BASIS] = jnp.where(across < SLOTS, near[0:BASIS], 0.0)
    wsum[...] = near[BASIS:]
    live_total = near[BASIS : BASIS + 1, WEIGHT : WEIGHT + 1]
    inverse = 1.0 / live_total
    factor_scale = lax.rsqrt(live_total)
    factor_scale = factor_scale * (1.5 - 0.5 * live_total * factor_scale * factor_scale)
    er[0 : BASIS + BLOCK] = gathered(along_genes, xs0, mine, g, s0s_sem, s0r_sem)

    def turned(column, start):
        return jnp.sum(jnp.where(lane == row + start, column, 0.0), axis=0, keepdims=True)

    def fresh(d):
        chigh, clow = split(chg[...])
        cboth = jnp.concatenate([chigh, clow], axis=0)
        return product(chigh, cboth, bhi[d, cells:], blo[d, cells:], ALONG)

    def emit(d, rows, values):
        @pl.when(d < whole)
        def _():
            right_out[rows, pl.ds(pl.multiple_of(d * width, LANES), width)] = values * scales[1]

        if spare:
            @pl.when(d == whole)
            def _():
                right_out[rows, whole * width : genes] = values[:, :spare] * scales[1]

    def update(j):
        later = pl.multiple_of(cells + BASIS + (j + 1) * BLOCK, BLOCK)
        rows = pl.ds(pl.multiple_of(j * BLOCK, BLOCK), BLOCK)

        def right(d):
            values = fresh(d)
            vhigh, vlow = split(values)
            bhi[d, pl.ds(later, BLOCK)] = vhigh
            blo[d, pl.ds(later, BLOCK)] = vlow
            emit(d, rows, values)

        loop(0, n, right)

    def keep(d, values):
        phigh, plow = split(values)
        bhi[d, cells + SLOTS : cells + SLOTS + BLOCK] = phigh
        blo[d, cells + SLOTS : cells + SLOTS + BLOCK] = plow
        return phigh, jnp.concatenate([phigh, plow], axis=0)

    def begin(j):
        @pl.when(j == 0)
        def _():
            base.third()

            def take(k):
                source = lax.rem(me + n - k, n)
                item = along_cells(tpart.at[source], tfrom.at[source], ts_sem.at[k], tr_sem.at[source], sibling)
                item.wait_send()
                item.wait_recv()
                tpart[me] = tpart[me] + tfrom[source]

            loop(1, n, take)
            stack[WEIGHT : WEIGHT + 1] = tpart[me]
            mr[0:BASIS] = gathered(along_genes, xb0, mine, g, b0s_sem, b0r_sem)

    def step(j, final):
        position = BASIS + j * BLOCK
        position = position if final else pl.multiple_of(position, BLOCK)
        mr[SLOTS : SLOTS + BLOCK] = gathered(along_genes, xg.at[j], mine, g, xs_sem.at[j], xr_sem.at[j])
        vectors = exact(chg[...], mr[...])
        mr[pl.ds(position, BLOCK)] = vectors
        sl[SLOTS : SLOTS + BLOCK] = vectors
        gram[me] = exact_rows(vectors, sl[...])
        spread(along_cells, gram, me, n, gs_sem, gr_sem)
        high, low = split(vectors)
        both = jnp.concatenate([high, low], axis=0)

        def produce(d):
            w[d] = product(high, both, bhi[d, 0:cells], blo[d, 0:cells], ALONG)

        walk.first(produce)
        walk.second(produce)
        if final:
            update(j - 1)
        else:
            begin(j)
            pl.when(j > 0)(lambda: update(j - 1))
        total = gathered(along_cells, gram, me, n, gs_sem, gr_sem)
        held = total[:, WEIGHT : WEIGHT + 1] * inverse
        weighed = wsum[0:1] + turned(total[:, WEIGHT : WEIGHT + 1], SLOTS)
        scale = jnp.where(lane < SLOTS, factor_scale, factor_scale * factor_scale)
        factor, against, change = orthonormal((total - held * weighed) * scale, el[...], tl[...])
        diag_out[j] = factor
        tilt = jnp.sum(jnp.where(lane < SLOTS, change * wsum[0:1], 0.0), axis=1, keepdims=True)
        wsum[0:1] = wsum[0:1] + turned(tilt, position)
        shift = jnp.sum(
            jnp.where((lane >= SLOTS) & (lane < WEIGHT), change * turned(held, SLOTS), 0.0), axis=1, keepdims=True
        )
        blend = jnp.where(
            lane < SLOTS, change,
            jnp.where(lane < WEIGHT, change * factor_scale, jnp.where(lane == WEIGHT, -shift * factor_scale, 0.0)),
        )
        leftvec = exact(blend, sl[...])
        sl[pl.ds(position, BLOCK)] = leftvec
        el[pl.ds(position, BLOCK)] = el[pl.ds(position, BLOCK)] + against
        tl[pl.ds(position, BLOCK)] = against
        left_out[pl.ds(position - BASIS, BLOCK)] = leftvec * scales[0]
        tilt = tilt * inverse
        blend = jnp.where(lane == WEIGHT, blend - tilt, blend) * factor_scale
        walk.third()
        if not final:
            pl.when(j == 0)(lambda: base.fourth(stack, slice(0, BASIS)))
        ground[...] = exact(jnp.where((lane < SLOTS) | (lane >= WEIGHT), blend, 0.0), stack[...])
        walk.fourth(stack, slice(SLOTS, SLOTS + BLOCK))
        columns = [blend[:, SLOTS + k : SLOTS + k + 1] for k in range(BLOCK)]
        for i in range(tiles):
            here = slice(i * LANES, (i + 1) * LANES)
            values = ground[:, here]
            for k in range(BLOCK):
                values = values + columns[k] * stack[SLOTS + k : SLOTS + k + 1, here]
            pb[me, :, here] = values

        def relay(z):
            t = z * b + yi
            d = 2 * t + core

            def to_y(k):
                y = lax.rem(yi + k, b)
                along_cells(pb.at[d], pb.at[d], fs_sem.at[z * b + y], cr_sem.at[d], 2 * (zi * b + y) + core).start()

            loop(1, b, to_y)
            along_cells(pb.at[d], pb.at[d], ds_sem.at[t], cr_sem.at[d], sibling).start()

        def arrived(d):
            along_cells(pb.at[d], pb.at[d], ds_sem.at[0], cr_sem.at[d], sibling).wait_recv()

        def go(k):
            z = lax.rem(zi + k, a)
            along_cells(pb.at[me], pb.at[me], cs_sem.at[z], cr_sem.at[me], 2 * (z * b + yi) + core).start()

        loop(1, a, go)
        relay(zi)
        phigh, pboth = keep(me, pb[me])
        gx[mine] = product(phigh, pboth, bhi[me, cells:], blo[me, cells:], ROWS)
        spread(along_genes, gx, mine, g, gxs_sem, gxr_sem)
        if not final:
            stack[pl.ds(position, BLOCK)] = (
                pb[me] * (live_total * factor_scale) + tilt * stack[WEIGHT : WEIGHT + 1]
            )
            xg[j + 1, mine] = jnp.zeros((BLOCK, LANES), F32)

        def consume(d):
            phigh, pboth = keep(d, pb[d])
            if final:
                emit(d, pl.ds((STEPS - 1) * BLOCK, BLOCK), fresh(d))
            else:
                xg[j + 1, mine] = xg[j + 1, mine] + product(phigh, pboth, bhi[d, 0:cells], blo[d, 0:cells], ROWS)

        def pass_z(k):
            z = lax.rem(zi + a - k, a)
            arrived(2 * (z * b + yi) + core)
            relay(z)

        seat = 2 * yi + core
        loop(1, min(2, a), pass_z)
        gy[seat] = gathered(along_genes, gx, mine, g, gxs_sem, gxr_sem)
        spread(along_plane, gy, seat, 2 * b, gys_sem, gyr_sem)
        loop(min(2, a), min(3, a), pass_z)
        gz[zi] = gathered(along_plane, gy, seat, 2 * b, gys_sem, gyr_sem)
        spread(along_column, gz, zi, a, gzs_sem, gzr_sem)
        loop(min(3, a), a, pass_z)

        def close():
            total = gathered(along_column, gz, zi, a, gzs_sem, gzr_sem)
            factor, against, change = orthonormal(total, er[...], tr[...])
            couple_out[j] = factor
            chg[...] = change
            if not final:
                later = pl.multiple_of(position + BLOCK, BLOCK)
                er[pl.ds(later, BLOCK)] = er[pl.ds(later, BLOCK)] + against
                tr[pl.ds(later, BLOCK)] = against

        if final:
            close()
        consume(me)
        loop(1, a, lambda k: consume(2 * (lax.rem(zi + a - k, a) * b + yi) + core))

        def pass_y(k):
            z = lax.rem(zi + a - lax.rem(k, a), a)
            t = z * b + lax.rem(yi + 1 + k // a, b)
            d = 2 * t + core
            arrived(d)
            along_cells(pb.at[d], pb.at[d], ds_sem.at[t], cr_sem.at[d], sibling).start()
            consume(d)

        loop(0, h - a, pass_y)

        def rest(k):
            z = lax.rem(zi + a - lax.rem(k, a), a)
            t = z * b + lax.rem(yi + k // a, b)
            d = 2 * t + 1 - core
            arrived(d)
            consume(d)

        loop(0, h, rest)
        if not final:
            spread(along_genes, xg.at[j + 1], mine, g, xs_sem.at[j + 1], xr_sem.at[j + 1])
            close()
        walk.ended()

        def ended(t):
            along_cells(pb.at[t], pb.at[t], ds_sem.at[t], cr_sem.at[t], sibling).wait_send()

        loop(0, h, ended)

        def ended_y(k):
            z, y = order(k)
            t = z * b + y
            along_cells(pb.at[t], pb.at[t], fs_sem.at[t], cr_sem.at[t], sibling).wait_send()

        loop(0, h - a, ended_y)

        def ended_z(k):
            z = lax.rem(zi + k, a)
            along_cells(pb.at[z], pb.at[z], cs_sem.at[z], cr_sem.at[z], sibling).wait_send()

        loop(1, a, ended_z)

    loop(0, STEPS - 1, lambda j: step(j, False))
    step(STEPS - 1, True)
    base.ended()


def body(counts, live_rows, left_basis, right_basis, right_start):
    cells, genes = counts.shape
    n = lax.axis_size("cells")
    g = lax.axis_size("genes")
    h = n // 2
    width = -(-(genes // LANES) // n) * LANES
    scales = (math.sqrt(float(cells * n)), math.sqrt(float(genes * g)))
    vmem = pl.BlockSpec(memory_space=pltpu.VMEM)
    anywhere = pl.BlockSpec(memory_space=pl.ANY)
    held = lambda *shape: pltpu.VMEM(shape, F32)
    square = held(LANES, LANES)
    dma = lambda *shape: pltpu.SemaphoreType.DMA(shape)
    out_shape = (
        jax.ShapeDtypeStruct((STEPS * BLOCK, cells), F32),
        jax.ShapeDtypeStruct((STEPS * BLOCK, genes), F32),
        jax.ShapeDtypeStruct((STEPS, BLOCK, BLOCK), F32),
        jax.ShapeDtypeStruct((STEPS, BLOCK, BLOCK), F32),
    )
    buffers = lambda rows: [
        held(n, rows, width), held(h, rows, width), held(h, rows, width), held(h, rows, width),
    ]
    scratch = [
        pltpu.VMEM((n, cells, width), jnp.int32),
        held(n, cells, width),
        pltpu.VMEM((n, cells + LANES, width), BF16),
        pltpu.VMEM((n, cells + LANES, width), BF16),
        held(n, BASIS + BLOCK, width),
        square, square, square, square, square, square,
        *buffers(BLOCK),
        *buffers(BASIS),
        held(n, BLOCK, width),
        held(LANES, width),
        held(BLOCK, width),
        held(n, 1, width),
        held(n, 1, width),
        held(n, 1, width),
        held(8, LANES),
        held(BLOCK, LANES),
        held(n, BASIS + 8, LANES),
        held(n, BLOCK, LANES),
        held(g, BASIS + BLOCK, LANES),
        held(g, BASIS, LANES),
        held(STEPS, g, BLOCK, LANES),
        held(g, BLOCK, LANES),
        held(n, BLOCK, LANES),
        held(h, BLOCK, LANES),
        dma(n, 3),
        *[dma(h)] * 6,
        *[dma(h)] * 6,
        dma(h), dma(n), dma(h), dma(h), dma(n), dma(n),
        *[dma(n)] * 6,
        *[dma(g)] * 4,
        dma(STEPS, g), dma(STEPS, g),
        dma(g), dma(g), dma(n), dma(n), dma(h), dma(h),
    ]
    return pl.pallas_call(
        functools.partial(kernel, n, g, width, scales),
        out_shape=out_shape,
        in_specs=[pl.BlockSpec(memory_space=pltpu.SMEM), anywhere, vmem, anywhere, anywhere],
        out_specs=(vmem, vmem, vmem, vmem),
        scratch_shapes=scratch,
        compiler_params=pltpu.CompilerParams(
            collective_id=0, has_side_effects=True, vmem_limit_bytes=66 * 1000 * 1000
        ),
    )(live_rows, counts, left_basis, right_basis, right_start)


def solution(mesh):
    in_specs = (
        P("cells", "genes"),
        P("cells"),
        P(None, "cells"),
        P(None, "genes"),
        P(None, "genes"),
    )
    out_specs = (P(None, "cells"), P(None, "genes"), P(), P())
    return jax.shard_map(body, mesh=mesh, in_specs=in_specs, out_specs=out_specs, check_vma=False)
```

time: 165 us -> 157 us (0.952)
  Pallas kernels: 157 us -> 149 us
    pallas_call x1, Pallas kernels: 157 us -> 149 us  [body(): pl.pallas_call(functools.partial(kernel, n, g, width, scales), out_shape=...]
where the time goes in v2:
time: 157 us
  Pallas kernels  149 us (95%)
  local copies, waits for them, and re-layouts  6.37 us (4%)
    pallas_call x1, Pallas kernels, body(): pl.pallas_call(functools.partial(kernel, n, g, width, scales), out_shape=...  149 us
    unnamed x8, local copies, waits for them, and re-layouts  6.37 us

profile of v2, /device:TPU:0, one launch (start us, length us, event | category | flops | bytes accessed | tf_op | source)
XLA Modules:
  0.0 157.1 jit_solution(9822434437032641618)
XLA Ops:
  1.3 149.5 %shard_map.84 = (f32[48,128]{1,0:T(8,128)}, f32[48,16640]{1,0:T(8,128)}, f32[3,16,16]{2,1,0:T(8,128)}, f32[3,16,16]{2,1,0:T(8,128)}) custom-call(s32[1]{0:T(128)S(6)} %copy.13.live, s32[128,16640]{1,0:T(8,128)} %counts.1, f32[32,128]{1,0:T(8,128)} %left_basis.1, f32[32,16640]{1,0:T(8,128)} %right_basis.1, f32[16,16640]{1,0:T(8,128)} %right_start.1), custom_call_target="tpu_custom_call" | custom-call | tf_op jit(solution)/shard_map/pallas_call | solution.py:652
  150.8 1.3 copy.14
  152.1 0.0 copy-start.1
  152.1 0.0 copy-start
  152.1 3.8 %copy.15 = f32[48,16640]{1,0:T(8,128)} copy(f32[48,16640]{1,0:T(8,128)} %get-tuple-element.9) | data formatting | bytes 6389760
  155.9 0.0 copy-done.1
  155.9 0.6 copy.16
  156.5 0.0 copy-done
  156.5 0.6 copy.17
Async XLA Ops:
  152.1 3.8 %copy-start.1 = (f32[3,16,16]{2,1,0:T(8,128)S(1)}, f32[3,16,16]{2,1,0:T(8,128)}, u32[]{:S(2)}) copy-start(f32[3,16,16]{2,1,0:T(8,128)} %get-tuple-element.10) | copy-start | bytes 9220
  152.1 4.4 %copy-start = (f32[3,16,16]{2,1,0:T(8,128)S(1)}, f32[3,16,16]{2,1,0:T(8,128)}, u32[]{:S(2)}) copy-start(f32[3,16,16]{2,1,0:T(8,128)} %get-tuple-element.11) | copy-start | bytes 9220

commit v3 on v2

--- a/solution.py
+++ b/solution.py
@@ -13,6 +13,7 @@
 STEPS = 3
 SLOTS = BASIS + STEPS * BLOCK
 WEIGHT = SLOTS + BLOCK
+LAG = 2
 LANES = 128
 F32 = jnp.float32
 BF16 = jnp.bfloat16
@@ -46,49 +47,52 @@
 ROWS = ((1,), (1,))
 
 
-def loop(start, stop, step):
+def loop(start, stop, step, unroll=1):
     def one(k, carry):
         step(k)
         return carry
 
-    lax.fori_loop(start, stop, one, 0)
-
-
-def orthonormal(gram, near, lower):
+    lax.fori_loop(start, stop, one, 0, unroll=unroll if (stop - start) % unroll == 0 else 1)
+
+
+def both_sides(gram, identity):
+    gap = identity - gram
+    return identity + gap, exact(gap, gap)
+
+
+def orthonormal(gram, first, second):
     lane = lax.broadcasted_iota(jnp.int32, (BLOCK, LANES), 1)
     row = lax.broadcasted_iota(jnp.int32, (BLOCK, LANES), 0)
     coeffs = jnp.where(lane < SLOTS, gram, 0.0)
-    squares = gram[:, SLOTS : SLOTS + BLOCK]
-    combined = coeffs + coeffs - (exact(coeffs, near) + exact_rows(coeffs, lower))
-    residue = coeffs - (exact(combined, near) + exact_rows(combined, lower))
-    squares = squares - exact_rows(combined, coeffs) - exact_rows(residue, combined)
+    combined = exact(coeffs, first)
+    residue = exact(coeffs, second)
+    squares = gram[:, SLOTS : SLOTS + BLOCK] - exact_rows(
+        jnp.concatenate([combined, residue], axis=1), jnp.concatenate([coeffs, combined], axis=1)
+    )
     change = jnp.where(lane == row + SLOTS, 1.0, -combined)
-    parts = [squares, residue, change]
+    columns = [jnp.broadcast_to(squares[:, k : k + 1], (BLOCK, LANES)) for k in range(BLOCK)]
+    factor = jnp.zeros((BLOCK, LANES), F32)
     for k in range(BLOCK):
-        pivot = parts[0][k : k + 1, k : k + 1]
+        pivot = jnp.broadcast_to(columns[k][k : k + 1], (BLOCK, LANES))
         root = lax.rsqrt(pivot)
         root = root * (1.5 - 0.5 * pivot * root * root)
-        column = parts[0][:, k : k + 1] * root
-        after = []
-        for part in parts:
-            scaled = part[k : k + 1, :] * root
-            places = lax.broadcasted_iota(jnp.int32, part.shape, 0)
-            after.append(
-                jnp.where(places > k, part - column * scaled, jnp.where(places == k, scaled, part))
-            )
-        parts = after
-    spot = lax.broadcasted_iota(jnp.int32, (BLOCK, BLOCK), 0)
-    other = lax.broadcasted_iota(jnp.int32, (BLOCK, BLOCK), 1)
-    upper = jnp.where(other >= spot, parts[0], 0.0)
-    factor = exact_rows(jnp.where(other == spot, 1.0, 0.0).astype(F32), upper)
-    return factor, parts[1], parts[2]
+        column = columns[k] * root
+        factor = jnp.where((lane == k) & (row >= k), column, factor)
+        below = jnp.where(row > k, column, 0.0)
+        for i in range(k + 1, BLOCK):
+            columns[i] = columns[i] - column * jnp.broadcast_to(column[i : i + 1], (BLOCK, LANES))
+        scaled = jnp.broadcast_to(residue[k : k + 1], (BLOCK, LANES)) * root
+        residue = jnp.where(row == k, scaled, residue - below * scaled)
+        scaled = jnp.broadcast_to(change[k : k + 1], (BLOCK, LANES)) * root
+        change = jnp.where(row == k, scaled, change - below * scaled)
+    return factor[:, :BLOCK], residue, change
 
 
 def kernel(
     n, g, width, scales,
     live, counts, left_basis, right_basis, right_start,
     left_out, right_out, diag_out, couple_out,
-    cnt, logged, bhi, blo, rb, sl, mr, el, tl, er, tr,
+    cnt, logged, lhi, llo, vhi, vlo, rb, sl, mr, el, er, l1, l2, r1, r2,
     w, ra, rt, rz, wb, rab, rtb, rzb, pb, stack, ground, tpart, tfrom,
     mu, wsum, chg, gram0, gram, xs0, xb0, xg, gx, gy, gz,
     in_sem, as_sem, ar_sem, bs_sem, br_sem, zs_sem, zr_sem,
@@ -182,8 +186,14 @@
             1, size, lambda k, total: total + buf[k], buf[0]
         )
 
+    def onward(k):
+        return lax.rem(zi + k, a)
+
+    def behind(k):
+        return lax.rem(zi + a - k, a)
+
     def order(k):
-        return lax.rem(zi + 1 + lax.rem(k, a), a), lax.rem(yi + 1 + k // a, b)
+        return onward(1 + lax.rem(k, a)), lax.rem(yi + 1 + k // a, b)
 
     class Scatter:
         def __init__(self, part, fromcore, fromy, fromz, sems):
@@ -193,33 +203,43 @@
         def over(self, d, t):
             return along_cells(self.part.at[d], self.fromcore.at[t], self.cs.at[t], self.cr.at[t], sibling)
 
-        def first(self, produce):
-            def one(k):
+        def launch(self, produce):
+            def other(k):
                 z, y = order(k)
                 t = z * b + y
-                d = 2 * t + 1 - core
-                produce(d)
-                self.over(d, t).start()
-
-            loop(0, h, one)
-
-        def second(self, produce):
-            def one(k, send):
+                return t, 2 * t + 1 - core
+
+            def own(k):
                 z, y = order(k)
                 t = z * b + y
-                d = 2 * t + core
-                produce(d)
+                return z, y, t, 2 * t + core
+
+            def join(k):
+                z, y, t, d = own(k)
                 self.over(d, t).wait_recv()
                 self.part[d] = self.part[d] + self.fromcore[t]
-                if send:
+
+                @pl.when(k < h - a)
+                def _():
                     to = z * b + yi
                     along_cells(
                         self.part.at[d], self.fromy.at[to], self.ys.at[t], self.yr.at[to],
                         2 * (zi * b + y) + core,
                     ).start()
 
-            loop(0, h - a, lambda k: one(k, True))
-            loop(h - a, h, lambda k: one(k, False))
+            def pair(k):
+                t, d = other(k)
+                produce(d)
+                produce(own(k)[3])
+                self.over(d, t).start()
+
+            def one(k):
+                pair(k)
+                join(k - LAG)
+
+            loop(0, LAG, pair)
+            loop(LAG, h, one)
+            loop(h - LAG, h, join)
 
         def complete(self, z):
             d = 2 * (z * b + yi) + core
@@ -232,20 +252,21 @@
             loop(1, b, add)
             return d
 
-        def third(self):
+        def third(self, start, stop):
             def one(k):
-                z = lax.rem(zi + k, a)
+                z = onward(1 + k)
                 d = self.complete(z)
                 along_cells(self.part.at[d], self.fromz.at[zi], self.zs.at[z], self.zr.at[zi], d).start()
 
-            loop(1, a, one)
-            self.complete(zi)
+            loop(min(start, a - 1), min(stop, a - 1), one)
+            if stop >= a:
+                self.complete(zi)
 
         def fourth(self, result, rows):
             result[rows] = self.part[me]
 
             def one(k):
-                z = lax.rem(zi + a - k, a)
+                z = behind(k)
                 along_cells(self.part.at[me], self.fromz.at[z], self.zs.at[z], self.zr.at[z], sibling).wait_recv()
                 result[rows] = result[rows] + self.fromz[z]
 
@@ -277,7 +298,7 @@
     weights = jnp.where(
         lax.broadcasted_iota(jnp.int32, (cells, LANES), 0) < live_here, 1.0, 0.0
     ).astype(F32)
-    for table in (sl, mr, tl, tr, stack):
+    for table in (sl, mr, stack):
         table[...] = jnp.zeros_like(table)
     same = jnp.where(
         lax.broadcasted_iota(jnp.int32, (LANES, LANES), 0)
@@ -286,6 +307,14 @@
     ).astype(F32)
     er[...] = same
     chg[...] = jnp.where(lane == row + SLOTS, 1.0, 0.0)
+
+    def extend(table, first, second, position, against):
+        here = jnp.where(lane == row + position, 1.0, 0.0).astype(F32)
+        turn = lambda lhs, rhs: lax.dot_general(
+            lhs, rhs, (((0,), (0,)), ((), ())), precision=HIGHEST, preferred_element_type=F32
+        )
+        table[...] = table[...] + turn(here, against) + turn(against, here)
+        first[...], second[...] = both_sides(table[...], same)
     sl[0:BASIS] = left_basis[...] * weights_row
     sl[WEIGHT : WEIGHT + 8] = jnp.where(
         lax.broadcasted_iota(jnp.int32, (8, cells), 0) == 0, weights_row, 0.0
@@ -319,16 +348,13 @@
 
     def fill(d):
         high, low = split(rb[d])
-        bhi[d, cells : cells + BASIS + BLOCK] = high
-        blo[d, cells : cells + BASIS + BLOCK] = low
+        vhi[d, 0 : BASIS + BLOCK] = high
+        vlo[d, 0 : BASIS + BLOCK] = low
         blank = jnp.zeros((LANES - BASIS - BLOCK, width), BF16)
-        bhi[d, cells + BASIS + BLOCK :] = blank
-        blo[d, cells + BASIS + BLOCK :] = blank
-        both = jnp.concatenate([high, low], axis=0)
-        xs0[mine] = xs0[mine] + product(high, both, bhi[d, cells:], blo[d, cells:], ROWS)
+        vhi[d, BASIS + BLOCK :] = blank
+        vlo[d, BASIS + BLOCK :] = blank
 
     loop(0, n, fill)
-    spread(along_genes, xs0, mine, g, s0s_sem, s0r_sem)
     waited(along_cells, mu, me, n, ms_sem, mr_sem)
 
     bhigh, blow = split(jnp.concatenate(
@@ -340,38 +366,44 @@
         for i in range(tiles):
             here = slice(i * LANES, (i + 1) * LANES)
             high, low = split(logged[d, :, here] - weights * mu[d, :, here])
-            bhi[d, 0:cells, here] = high
-            blo[d, 0:cells, here] = low
-        high = bhi[d, cells : cells + BASIS + BLOCK]
-        both = jnp.concatenate([high, blo[d, cells : cells + BASIS + BLOCK]], axis=0)
-        met = product(high, both, bhi[d, 0:cells], blo[d, 0:cells], ROWS)
-        xb0[mine] = xb0[mine] + met[0:BASIS]
-        xg[0, mine] = xg[0, mine] + met[BASIS:]
-        made = product(bhigh, bboth, bhi[d, 0:cells], blo[d, 0:cells], ALONG)
+            lhi[d, :, here] = high
+            llo[d, :, here] = low
+        made = product(bhigh, bboth, lhi[d], llo[d], ALONG)
         wb[d] = made[0:BASIS]
         tpart[d] = made[BASIS : BASIS + 1]
 
-    base.first(center)
-    base.second(center)
-    spread(along_genes, xg.at[0], mine, g, xs_sem.at[0], xr_sem.at[0])
-    spread(along_genes, xb0, mine, g, b0s_sem, b0r_sem)
+    base.launch(center)
 
     def give(k):
         d = lax.rem(me + k, n)
         along_cells(tpart.at[d], tfrom.at[me], ts_sem.at[k], tr_sem.at[me], d).start()
 
     loop(1, n, give)
+
+    def cross(d):
+        high = vhi[d, 0 : BASIS + BLOCK]
+        both = jnp.concatenate([high, vlo[d, 0 : BASIS + BLOCK]], axis=0)
+        met = product(high, both, lhi[d], llo[d], ROWS)
+        xb0[mine] = xb0[mine] + met[0:BASIS]
+        xg[0, mine] = xg[0, mine] + met[BASIS:]
+
+    base.third(0, 1)
+    loop(0, n, cross, 2)
+    spread(along_genes, xg.at[0], mine, g, xs_sem.at[0], xr_sem.at[0])
+    spread(along_genes, xb0, mine, g, b0s_sem, b0r_sem)
+    base.third(1, 2)
+
     near = gathered(along_cells, gram0, me, n, g0s_sem, g0r_sem)
     corner = lax.broadcasted_iota(jnp.int32, (LANES, LANES), 0)
     across = lax.broadcasted_iota(jnp.int32, (BASIS, LANES), 1)
     el[...] = jnp.where((same > 0) & (corner >= BASIS), 1.0, 0.0)
     el[0:BASIS] = jnp.where(across < SLOTS, near[0:BASIS], 0.0)
+    l1[...], l2[...] = both_sides(el[...], same)
     wsum[...] = near[BASIS:]
     live_total = near[BASIS : BASIS + 1, WEIGHT : WEIGHT + 1]
     inverse = 1.0 / live_total
     factor_scale = lax.rsqrt(live_total)
     factor_scale = factor_scale * (1.5 - 0.5 * live_total * factor_scale * factor_scale)
-    er[0 : BASIS + BLOCK] = gathered(along_genes, xs0, mine, g, s0s_sem, s0r_sem)
 
     def turned(column, start):
         return jnp.sum(jnp.where(lane == row + start, column, 0.0), axis=0, keepdims=True)
@@ -379,7 +411,7 @@
     def fresh(d):
         chigh, clow = split(chg[...])
         cboth = jnp.concatenate([chigh, clow], axis=0)
-        return product(chigh, cboth, bhi[d, cells:], blo[d, cells:], ALONG)
+        return product(chigh, cboth, vhi[d], vlo[d], ALONG)
 
     def emit(d, rows, values):
         @pl.when(d < whole)
@@ -391,40 +423,35 @@
             def _():
                 right_out[rows, whole * width : genes] = values[:, :spare] * scales[1]
 
-    def update(j):
-        later = pl.multiple_of(cells + BASIS + (j + 1) * BLOCK, BLOCK)
+    def update(j, start, stop):
+        later = pl.multiple_of(BASIS + (j + 1) * BLOCK, BLOCK)
         rows = pl.ds(pl.multiple_of(j * BLOCK, BLOCK), BLOCK)
 
         def right(d):
             values = fresh(d)
             vhigh, vlow = split(values)
-            bhi[d, pl.ds(later, BLOCK)] = vhigh
-            blo[d, pl.ds(later, BLOCK)] = vlow
+            vhi[d, pl.ds(later, BLOCK)] = vhigh
+            vlo[d, pl.ds(later, BLOCK)] = vlow
             emit(d, rows, values)
 
-        loop(0, n, right)
+        loop(start, stop, right)
 
     def keep(d, values):
         phigh, plow = split(values)
-        bhi[d, cells + SLOTS : cells + SLOTS + BLOCK] = phigh
-        blo[d, cells + SLOTS : cells + SLOTS + BLOCK] = plow
+        vhi[d, SLOTS : SLOTS + BLOCK] = phigh
+        vlo[d, SLOTS : SLOTS + BLOCK] = plow
         return phigh, jnp.concatenate([phigh, plow], axis=0)
+
+    def meet(d):
+        high = vhi[d, 0 : BASIS + BLOCK]
+        both = jnp.concatenate([high, vlo[d, 0 : BASIS + BLOCK]], axis=0)
+        xs0[mine] = xs0[mine] + product(high, both, vhi[d], vlo[d], ROWS)
 
     def begin(j):
         @pl.when(j == 0)
         def _():
-            base.third()
-
-            def take(k):
-                source = lax.rem(me + n - k, n)
-                item = along_cells(tpart.at[source], tfrom.at[source], ts_sem.at[k], tr_sem.at[source], sibling)
-                item.wait_send()
-                item.wait_recv()
-                tpart[me] = tpart[me] + tfrom[source]
-
-            loop(1, n, take)
-            stack[WEIGHT : WEIGHT + 1] = tpart[me]
-            mr[0:BASIS] = gathered(along_genes, xb0, mine, g, b0s_sem, b0r_sem)
+            base.third(2, a)
+            walk.third(0, 2)
 
     def step(j, final):
         position = BASIS + j * BLOCK
@@ -439,20 +466,29 @@
         both = jnp.concatenate([high, low], axis=0)
 
         def produce(d):
-            w[d] = product(high, both, bhi[d, 0:cells], blo[d, 0:cells], ALONG)
-
-        walk.first(produce)
-        walk.second(produce)
+            w[d] = product(high, both, lhi[d], llo[d], ALONG)
+
+        walk.launch(produce)
         if final:
-            update(j - 1)
+            update(j - 1, 0, n // 2)
+            walk.third(0, 1)
+            update(j - 1, n // 2, n)
+            walk.third(1, 2)
         else:
             begin(j)
-            pl.when(j > 0)(lambda: update(j - 1))
+
+            @pl.when(j > 0)
+            def _():
+                update(j - 1, 0, n // 2)
+                walk.third(0, 1)
+                update(j - 1, n // 2, n)
+                walk.third(1, 2)
+
         total = gathered(along_cells, gram, me, n, gs_sem, gr_sem)
         held = total[:, WEIGHT : WEIGHT + 1] * inverse
         weighed = wsum[0:1] + turned(total[:, WEIGHT : WEIGHT + 1], SLOTS)
         scale = jnp.where(lane < SLOTS, factor_scale, factor_scale * factor_scale)
-        factor, against, change = orthonormal((total - held * weighed) * scale, el[...], tl[...])
+        factor, against, change = orthonormal((total - held * weighed) * scale, l1[...], l2[...])
         diag_out[j] = factor
         tilt = jnp.sum(jnp.where(lane < SLOTS, change * wsum[0:1], 0.0), axis=1, keepdims=True)
         wsum[0:1] = wsum[0:1] + turned(tilt, position)
@@ -465,15 +501,35 @@
         )
         leftvec = exact(blend, sl[...])
         sl[pl.ds(position, BLOCK)] = leftvec
-        el[pl.ds(position, BLOCK)] = el[pl.ds(position, BLOCK)] + against
-        tl[pl.ds(position, BLOCK)] = against
         left_out[pl.ds(position - BASIS, BLOCK)] = leftvec * scales[0]
         tilt = tilt * inverse
         blend = jnp.where(lane == WEIGHT, blend - tilt, blend) * factor_scale
-        walk.third()
+
+        def settle():
+            ground[...] = exact(jnp.where((lane < SLOTS) | (lane >= WEIGHT), blend, 0.0), stack[...])
+
+        if final:
+            settle()
+        else:
+            pl.when(j > 0)(settle)
+        walk.third(2, a)
         if not final:
-            pl.when(j == 0)(lambda: base.fourth(stack, slice(0, BASIS)))
-        ground[...] = exact(jnp.where((lane < SLOTS) | (lane >= WEIGHT), blend, 0.0), stack[...])
+            @pl.when(j == 0)
+            def _():
+                base.fourth(stack, slice(0, BASIS))
+
+                def take(k):
+                    source = lax.rem(me + n - k, n)
+                    item = along_cells(tpart.at[source], tfrom.at[source], ts_sem.at[k], tr_sem.at[source], sibling)
+                    item.wait_send()
+                    item.wait_recv()
+                    tpart[me] = tpart[me] + tfrom[source]
+
+                loop(1, n, take)
+                stack[WEIGHT : WEIGHT + 1] = tpart[me]
+                settle()
+                mr[0:BASIS] = gathered(along_genes, xb0, mine, g, b0s_sem, b0r_sem)
+
         walk.fourth(stack, slice(SLOTS, SLOTS + BLOCK))
         columns = [blend[:, SLOTS + k : SLOTS + k + 1] for k in range(BLOCK)]
         for i in range(tiles):
@@ -498,74 +554,105 @@
             along_cells(pb.at[d], pb.at[d], ds_sem.at[0], cr_sem.at[d], sibling).wait_recv()
 
         def go(k):
-            z = lax.rem(zi + k, a)
+            z = onward(k)
             along_cells(pb.at[me], pb.at[me], cs_sem.at[z], cr_sem.at[me], 2 * (z * b + yi) + core).start()
 
-        loop(1, a, go)
-        relay(zi)
+        if not final:
+            loop(1, min(2, a), go)
+            relay(zi)
         phigh, pboth = keep(me, pb[me])
-        gx[mine] = product(phigh, pboth, bhi[me, cells:], blo[me, cells:], ROWS)
-        spread(along_genes, gx, mine, g, gxs_sem, gxr_sem)
+        gz[zi] = product(phigh, pboth, vhi[me], vlo[me], ROWS)
+        spread(along_column, gz, zi, a, gzs_sem, gzr_sem)
+        if final:
+            loop(1, min(2, a), go)
+            relay(zi)
+        loop(min(2, a), a, go)
         if not final:
             stack[pl.ds(position, BLOCK)] = (
                 pb[me] * (live_total * factor_scale) + tilt * stack[WEIGHT : WEIGHT + 1]
             )
             xg[j + 1, mine] = jnp.zeros((BLOCK, LANES), F32)
+            extend(el, l1, l2, position, against)
 
         def consume(d):
             phigh, pboth = keep(d, pb[d])
             if final:
                 emit(d, pl.ds((STEPS - 1) * BLOCK, BLOCK), fresh(d))
             else:
-                xg[j + 1, mine] = xg[j + 1, mine] + product(phigh, pboth, bhi[d, 0:cells], blo[d, 0:cells], ROWS)
+                xg[j + 1, mine] = xg[j + 1, mine] + product(phigh, pboth, lhi[d], llo[d], ROWS)
 
         def pass_z(k):
-            z = lax.rem(zi + a - k, a)
+            z = behind(k)
             arrived(2 * (z * b + yi) + core)
             relay(z)
 
         seat = 2 * yi + core
+        def quarter(q):
+            if not final:
+                pl.when(j == 0)(lambda: loop(q * n // 4, (q + 1) * n // 4, meet))
+
+        quarter(0)
         loop(1, min(2, a), pass_z)
-        gy[seat] = gathered(along_genes, gx, mine, g, gxs_sem, gxr_sem)
-        spread(along_plane, gy, seat, 2 * b, gys_sem, gyr_sem)
-        loop(min(2, a), min(3, a), pass_z)
-        gz[zi] = gathered(along_plane, gy, seat, 2 * b, gys_sem, gyr_sem)
-        spread(along_column, gz, zi, a, gzs_sem, gzr_sem)
+        quarter(1)
+        if not final:
+            loop(min(2, a), min(3, a), pass_z)
+        gx[mine] = gathered(along_column, gz, zi, a, gzs_sem, gzr_sem)
+        spread(along_genes, gx, mine, g, gxs_sem, gxr_sem)
+        if final:
+            loop(min(2, a), min(3, a), pass_z)
+        quarter(2)
         loop(min(3, a), a, pass_z)
+        quarter(3)
+        if not final:
+            pl.when(j == 0)(lambda: spread(along_genes, xs0, mine, g, s0s_sem, s0r_sem))
+
+        def plane():
+            gy[seat] = gathered(along_genes, gx, mine, g, gxs_sem, gxr_sem)
+            spread(along_plane, gy, seat, 2 * b, gys_sem, gyr_sem)
+
+        def open_right():
+            met = gathered(along_genes, xs0, mine, g, s0s_sem, s0r_sem)
+            held = lax.broadcasted_iota(jnp.int32, met.shape, 1) < SLOTS
+            er[0 : BASIS + BLOCK] = jnp.where(held, met, 0.0)
+            r1[...], r2[...] = both_sides(er[...], same)
 
         def close():
-            total = gathered(along_column, gz, zi, a, gzs_sem, gzr_sem)
-            factor, against, change = orthonormal(total, er[...], tr[...])
+            if not final:
+                pl.when(j == 0)(open_right)
+            total = gathered(along_plane, gy, seat, 2 * b, gys_sem, gyr_sem)
+            factor, against, change = orthonormal(total, r1[...], r2[...])
             couple_out[j] = factor
             chg[...] = change
             if not final:
-                later = pl.multiple_of(position + BLOCK, BLOCK)
-                er[pl.ds(later, BLOCK)] = er[pl.ds(later, BLOCK)] + against
-                tr[pl.ds(later, BLOCK)] = against
+                extend(er, r1, r2, position + BLOCK, against)
 
         if final:
+            plane()
             close()
         consume(me)
-        loop(1, a, lambda k: consume(2 * (lax.rem(zi + a - k, a) * b + yi) + core))
+        loop(1, a, lambda k: consume(2 * (behind(k) * b + yi) + core))
 
         def pass_y(k):
-            z = lax.rem(zi + a - lax.rem(k, a), a)
+            z = behind(lax.rem(k, a))
             t = z * b + lax.rem(yi + 1 + k // a, b)
             d = 2 * t + core
             arrived(d)
             along_cells(pb.at[d], pb.at[d], ds_sem.at[t], cr_sem.at[d], sibling).start()
             consume(d)
 
-        loop(0, h - a, pass_y)
-
         def rest(k):
-            z = lax.rem(zi + a - lax.rem(k, a), a)
+            z = behind(lax.rem(k, a))
             t = z * b + lax.rem(yi + k // a, b)
             d = 2 * t + 1 - core
             arrived(d)
             consume(d)
 
-        loop(0, h, rest)
+        if not final:
+            plane()
+        loop(0, a, rest)
+        loop(0, h - a, pass_y)
+
+        loop(a, h, rest)
         if not final:
             spread(along_genes, xg.at[j + 1], mine, g, xs_sem.at[j + 1], xr_sem.at[j + 1])
             close()
@@ -618,10 +705,10 @@
     scratch = [
         pltpu.VMEM((n, cells, width), jnp.int32),
         held(n, cells, width),
-        pltpu.VMEM((n, cells + LANES, width), BF16),
-        pltpu.VMEM((n, cells + LANES, width), BF16),
+        *[pltpu.VMEM((n, cells, width), BF16)] * 2,
+        *[pltpu.VMEM((n, LANES, width), BF16)] * 2,
         held(n, BASIS + BLOCK, width),
-        square, square, square, square, square, square,
+        *[square] * 8,
         *buffers(BLOCK),
         *buffers(BASIS),
         held(n, BLOCK, width),

time: 157 us -> 145 us (0.924)
  Pallas kernels: 149 us -> 137 us
    pallas_call x1, Pallas kernels: 149 us -> 137 us  [body(): pl.pallas_call(functools.partial(kernel, n, g, width, scales), out_shape=...]
where the time goes in v3:
time: 145 us
  Pallas kernels  137 us (94%)
  local copies, waits for them, and re-layouts  6.37 us (4%)
    pallas_call x1, Pallas kernels, body(): pl.pallas_call(functools.partial(kernel, n, g, width, scales), out_shape=...  137 us
    unnamed x8, local copies, waits for them, and re-layouts  6.37 us

profile of v3, /device:TPU:0, one launch (start us, length us, event | category | flops | bytes accessed | tf_op | source)
XLA Modules:
  0.0 144.7 jit_solution(4598625761304378926)
XLA Ops:
  1.3 137.0 %shard_map.84 = (f32[48,128]{1,0:T(8,128)}, f32[48,16640]{1,0:T(8,128)}, f32[3,16,16]{2,1,0:T(8,128)}, f32[3,16,16]{2,1,0:T(8,128)}) custom-call(s32[1]{0:T(128)S(6)} %copy.13.live, s32[128,16640]{1,0:T(8,128)} %counts.1, f32[32,128]{1,0:T(8,128)} %left_basis.1, f32[32,16640]{1,0:T(8,128)} %right_basis.1, f32[16,16640]{1,0:T(8,128)} %right_start.1), custom_call_target="tpu_custom_call" | custom-call | tf_op jit(solution)/shard_map/pallas_call | solution.py:739
  138.3 1.3 copy.14
  139.7 0.0 copy-start.1
  139.7 0.0 copy-start
  139.7 3.8 %copy.15 = f32[48,16640]{1,0:T(8,128)} copy(f32[48,16640]{1,0:T(8,128)} %get-tuple-element.9) | data formatting | bytes 6389760
  143.5 0.0 copy-done.1
  143.5 0.6 copy.16
  144.1 0.0 copy-done
  144.1 0.6 copy.17
Async XLA Ops:
  139.7 3.8 %copy-start.1 = (f32[3,16,16]{2,1,0:T(8,128)S(1)}, f32[3,16,16]{2,1,0:T(8,128)}, u32[]{:S(2)}) copy-start(f32[3,16,16]{2,1,0:T(8,128)} %get-tuple-element.10) | copy-start | bytes 9220
  139.7 4.4 %copy-start = (f32[3,16,16]{2,1,0:T(8,128)S(1)}, f32[3,16,16]{2,1,0:T(8,128)}, u32[]{:S(2)}) copy-start(f32[3,16,16]{2,1,0:T(8,128)} %get-tuple-element.11) | copy-start | bytes 9220

commit v4 on v3

--- a/solution.py
+++ b/solution.py
@@ -88,18 +88,24 @@
     return factor[:, :BLOCK], residue, change
 
 
+def chunks(n, genes):
+    brief, extra = divmod(genes // LANES, n)
+    stride = n // extra if extra else n
+    return brief, [i * stride + (2 * (i % 2) if stride > 3 else 0) for i in range(extra)]
+
+
 def kernel(
     n, g, width, scales,
     live, counts, left_basis, right_basis, right_start,
-    left_out, right_out, diag_out, couple_out,
-    cnt, logged, lhi, llo, vhi, vlo, rb, sl, mr, el, er, l1, l2, r1, r2,
+    left_out, right_hbm, diag_out, couple_out,
+    right_out, cnt, logged, lhi, llo, vhi, vlo, rb, sl, mr, el, er, l1, l2, r1, r2,
     w, ra, rt, rz, wb, rab, rtb, rzb, pb, stack, ground, tpart, tfrom,
     mu, wsum, chg, gram0, gram, xs0, xb0, xg, gx, gy, gz,
     in_sem, as_sem, ar_sem, bs_sem, br_sem, zs_sem, zr_sem,
     bas_sem, bar_sem, bbs_sem, bbr_sem, bzs_sem, bzr_sem,
     cs_sem, cr_sem, ds_sem, fs_sem, ts_sem, tr_sem,
     ms_sem, mr_sem, g0s_sem, g0r_sem, gs_sem, gr_sem, s0s_sem, s0r_sem, b0s_sem, b0r_sem,
-    xs_sem, xr_sem, gxs_sem, gxr_sem, gys_sem, gyr_sem, gzs_sem, gzr_sem,
+    xs_sem, xr_sem, gxs_sem, gxr_sem, gys_sem, gyr_sem, gzs_sem, gzr_sem, out_sem, tail_sem,
 ):
     cells, genes = counts.shape
     me = lax.axis_index("cells")
@@ -113,7 +119,8 @@
     zi, yi = chip // b, lax.rem(chip, b)
     sibling = me + 1 - 2 * core
     tiles = width // LANES
-    whole, spare = genes // width, genes % width
+    brief, longs = chunks(n, genes)
+    brief = brief * LANES
     lane = lax.broadcasted_iota(jnp.int32, (BLOCK, LANES), 1)
     row = lax.broadcasted_iota(jnp.int32, (BLOCK, LANES), 0)
 
@@ -135,24 +142,67 @@
     def along_column(src, dst, send, recv, peer):
         return along_cells(src, dst, send, recv, 2 * (peer * b + yi) + core)
 
-    loads = []
-    for d in range(n):
-        cols = max(0, min(width, genes - d * width))
-        if cols:
-            here = pl.ds(d * width, cols)
-            loads.append((d, [
-                pltpu.make_async_copy(counts.at[:, here], cnt.at[d, :, pl.ds(0, cols)], in_sem.at[d, 0]),
-                pltpu.make_async_copy(right_basis.at[:, here], rb.at[d, pl.ds(0, BASIS), pl.ds(0, cols)], in_sem.at[d, 1]),
-                pltpu.make_async_copy(right_start.at[:, here], rb.at[d, pl.ds(BASIS, BLOCK), pl.ds(0, cols)], in_sem.at[d, 2]),
-            ]))
-        if cols < width:
-            cnt[d, :, cols:] = jnp.zeros((cells, width - cols), jnp.int32)
-            rb[d, :, cols:] = jnp.zeros((BASIS + BLOCK, width - cols), F32)
-    for _, trio in loads:
-        trio[0].start()
-    for _, trio in loads:
-        trio[1].start()
-        trio[2].start()
+    def is_long(d):
+        found = d == longs[0]
+        for other in longs[1:]:
+            found = found | (d == other)
+        return found
+
+    def first_gene(d):
+        at = d * brief
+        for other in longs:
+            at = at + jnp.where(d > other, LANES, 0)
+        return pl.multiple_of(at, LANES)
+
+    def fill_in(d, kind, method):
+        here, there, rows = (
+            (counts, cnt, pl.ds(0, cells)), (right_basis, rb, pl.ds(0, BASIS)), (right_start, rb, pl.ds(BASIS, BLOCK)),
+        )[kind]
+        at = first_gene(d)
+        getattr(pltpu.make_async_copy(
+            here.at[:, pl.ds(at, brief)], there.at[d, rows, pl.ds(0, brief)], in_sem.at[d, kind, 0]
+        ), method)()
+        if longs:
+            @pl.when(is_long(d))
+            def _():
+                getattr(pltpu.make_async_copy(
+                    here.at[:, pl.ds(pl.multiple_of(at + brief, LANES), LANES)],
+                    there.at[d, rows, pl.ds(brief, LANES)], in_sem.at[d, kind, 1],
+                ), method)()
+
+    def hop(src, dst, send, recv, peer, d):
+        def act(method):
+            getattr(along_cells(
+                src.at[:, pl.ds(0, brief)], dst.at[:, pl.ds(0, brief)],
+                send[0].at[0, send[1]], recv[0].at[0, recv[1]], peer,
+            ), method)()
+            if longs:
+                @pl.when(is_long(d))
+                def _():
+                    getattr(along_cells(
+                        src.at[:, pl.ds(brief, LANES)], dst.at[:, pl.ds(brief, LANES)],
+                        send[0].at[1, send[1]], recv[0].at[1, recv[1]], peer,
+                    ), method)()
+
+        return act
+
+    def around(k):
+        return lax.rem(me + k, n)
+
+    loop(0, n, lambda k: fill_in(around(k), 0, "start"))
+
+    def more(k):
+        fill_in(around(k), 1, "start")
+        fill_in(around(k), 2, "start")
+
+    loop(0, n, more)
+    if longs:
+        for d in range(n):
+            if d not in longs:
+                cnt[d, :, brief:] = jnp.zeros((cells, LANES), jnp.int32)
+                rb[d, :, brief:] = jnp.zeros((BASIS + BLOCK, LANES), F32)
+        for table in (ra, rt, rz, rab, rtb, rzb, pb):
+            table[:, :, brief:] = jnp.zeros((table.shape[0], table.shape[1], LANES), F32)
 
     barrier = pltpu.get_barrier_semaphore()
 
@@ -201,7 +251,7 @@
             self.cs, self.cr, self.ys, self.yr, self.zs, self.zr = sems
 
         def over(self, d, t):
-            return along_cells(self.part.at[d], self.fromcore.at[t], self.cs.at[t], self.cr.at[t], sibling)
+            return hop(self.part.at[d], self.fromcore.at[t], (self.cs, t), (self.cr, t), sibling, d)
 
         def launch(self, produce):
             def other(k):
@@ -216,22 +266,22 @@
 
             def join(k):
                 z, y, t, d = own(k)
-                self.over(d, t).wait_recv()
+                self.over(d, t)("wait_recv")
                 self.part[d] = self.part[d] + self.fromcore[t]
 
                 @pl.when(k < h - a)
                 def _():
                     to = z * b + yi
-                    along_cells(
-                        self.part.at[d], self.fromy.at[to], self.ys.at[t], self.yr.at[to],
-                        2 * (zi * b + y) + core,
-                    ).start()
+                    hop(
+                        self.part.at[d], self.fromy.at[to], (self.ys, t), (self.yr, to),
+                        2 * (zi * b + y) + core, d,
+                    )("start")
 
             def pair(k):
                 t, d = other(k)
                 produce(d)
                 produce(own(k)[3])
-                self.over(d, t).start()
+                self.over(d, t)("start")
 
             def one(k):
                 pair(k)
@@ -246,7 +296,7 @@
 
             def add(k):
                 source = z * b + lax.rem(yi + k, b)
-                along_cells(self.part.at[d], self.fromy.at[source], self.ys.at[source], self.yr.at[source], sibling).wait_recv()
+                hop(self.part.at[d], self.fromy.at[source], (self.ys, source), (self.yr, source), sibling, d)("wait_recv")
                 self.part[d] = self.part[d] + self.fromy[source]
 
             loop(1, b, add)
@@ -256,7 +306,7 @@
             def one(k):
                 z = onward(1 + k)
                 d = self.complete(z)
-                along_cells(self.part.at[d], self.fromz.at[zi], self.zs.at[z], self.zr.at[zi], d).start()
+                hop(self.part.at[d], self.fromz.at[zi], (self.zs, z), (self.zr, zi), d, d)("start")
 
             loop(min(start, a - 1), min(stop, a - 1), one)
             if stop >= a:
@@ -267,24 +317,25 @@
 
             def one(k):
                 z = behind(k)
-                along_cells(self.part.at[me], self.fromz.at[z], self.zs.at[z], self.zr.at[z], sibling).wait_recv()
+                hop(self.part.at[me], self.fromz.at[z], (self.zs, z), (self.zr, z), sibling, me)("wait_recv")
                 result[rows] = result[rows] + self.fromz[z]
 
             loop(1, a, one)
 
         def ended(self):
-            loop(0, h, lambda t: self.over(t, t).wait_send())
+            loop(0, h, lambda t: self.over(2 * t + 1 - core, t)("wait_send"))
 
             def sent_y(k):
                 z, y = order(k)
                 t = z * b + y
-                along_cells(self.part.at[t], self.fromy.at[t], self.ys.at[t], self.yr.at[t], sibling).wait_send()
+                hop(self.part.at[t], self.fromy.at[t], (self.ys, t), (self.yr, t), sibling, 2 * t + core)("wait_send")
 
             loop(0, h - a, sent_y)
 
             def sent_z(k):
                 z = lax.rem(zi + k, a)
-                along_cells(self.part.at[z], self.fromz.at[z], self.zs.at[z], self.zr.at[z], sibling).wait_send()
+                d = 2 * (z * b + yi) + core
+                hop(self.part.at[z], self.fromz.at[z], (self.zs, z), (self.zr, z), sibling, d)("wait_send")
 
             loop(1, a, sent_z)
 
@@ -327,8 +378,7 @@
             here = slice(i * LANES, (i + 1) * LANES)
             logged[d, :, here] = jnp.log(1.0 + cnt[d, :, here].astype(F32)) * weights
 
-    for _, trio in loads:
-        trio[0].wait()
+    fill_in(me, 0, "wait")
     take_log(me)
     portion = 1.0 / jnp.maximum(live_here, 1).astype(F32)
     for i in range(tiles):
@@ -337,16 +387,20 @@
     pl.semaphore_wait(barrier, n - 1 + g - 1)
     spread(along_cells, mu, me, n, ms_sem, mr_sem)
     spread(along_cells, gram0, me, n, g0s_sem, g0r_sem)
-    loop(1, n, lambda k: take_log(lax.rem(me + k, n)))
-
-    for _, trio in loads:
-        trio[1].wait()
-        trio[2].wait()
+
+    def next_log(k):
+        fill_in(around(k), 0, "wait")
+        take_log(around(k))
+
+    loop(1, n, next_log)
     xs0[mine] = jnp.zeros((BASIS + BLOCK, LANES), F32)
     xb0[mine] = jnp.zeros((BASIS, LANES), F32)
     xg[0, mine] = jnp.zeros((BLOCK, LANES), F32)
 
-    def fill(d):
+    def fill(k):
+        d = around(k)
+        fill_in(d, 1, "wait")
+        fill_in(d, 2, "wait")
         high, low = split(rb[d])
         vhi[d, 0 : BASIS + BLOCK] = high
         vlo[d, 0 : BASIS + BLOCK] = low
@@ -414,14 +468,31 @@
         return product(chigh, cboth, vhi[d], vlo[d], ALONG)
 
     def emit(d, rows, values):
-        @pl.when(d < whole)
-        def _():
-            right_out[rows, pl.ds(pl.multiple_of(d * width, LANES), width)] = values * scales[1]
-
-        if spare:
-            @pl.when(d == whole)
+        values = values * scales[1]
+        at = first_gene(d)
+        right_out[rows, pl.ds(at, brief)] = values[:, :brief]
+        if longs:
+            @pl.when(is_long(d))
             def _():
-                right_out[rows, whole * width : genes] = values[:, :spare] * scales[1]
+                right_out[rows, pl.ds(pl.multiple_of(at + brief, LANES), LANES)] = values[:, brief:]
+
+    def shipped(d, method):
+        rows = pl.ds((STEPS - 1) * BLOCK, BLOCK)
+        at = first_gene(d)
+
+        def act(start, size, which):
+            here = pl.ds(start, size)
+            getattr(pltpu.make_async_copy(
+                right_out.at[rows, here], right_hbm.at[rows, here], tail_sem.at[d, which]
+            ), method)()
+
+        act(at, brief, 0)
+        if longs:
+            pl.when(is_long(d))(lambda: act(pl.multiple_of(at + brief, LANES), LANES, 1))
+
+    def block(j):
+        rows = pl.ds(j * BLOCK if isinstance(j, int) else pl.multiple_of(j * BLOCK, BLOCK), BLOCK)
+        return pltpu.make_async_copy(right_out.at[rows], right_hbm.at[rows], out_sem.at[j])
 
     def update(j, start, stop):
         later = pl.multiple_of(BASIS + (j + 1) * BLOCK, BLOCK)
@@ -473,6 +544,7 @@
             update(j - 1, 0, n // 2)
             walk.third(0, 1)
             update(j - 1, n // 2, n)
+            block(j - 1).start()
             walk.third(1, 2)
         else:
             begin(j)
@@ -482,6 +554,7 @@
                 update(j - 1, 0, n // 2)
                 walk.third(0, 1)
                 update(j - 1, n // 2, n)
+                block(j - 1).start()
                 walk.third(1, 2)
 
         total = gathered(along_cells, gram, me, n, gs_sem, gr_sem)
@@ -489,6 +562,7 @@
         weighed = wsum[0:1] + turned(total[:, WEIGHT : WEIGHT + 1], SLOTS)
         scale = jnp.where(lane < SLOTS, factor_scale, factor_scale * factor_scale)
         factor, against, change = orthonormal((total - held * weighed) * scale, l1[...], l2[...])
+        walk.third(2, a - 1)
         diag_out[j] = factor
         tilt = jnp.sum(jnp.where(lane < SLOTS, change * wsum[0:1], 0.0), axis=1, keepdims=True)
         wsum[0:1] = wsum[0:1] + turned(tilt, position)
@@ -512,7 +586,7 @@
             settle()
         else:
             pl.when(j > 0)(settle)
-        walk.third(2, a)
+        walk.third(a - 1, a)
         if not final:
             @pl.when(j == 0)
             def _():
@@ -545,29 +619,30 @@
 
             def to_y(k):
                 y = lax.rem(yi + k, b)
-                along_cells(pb.at[d], pb.at[d], fs_sem.at[z * b + y], cr_sem.at[d], 2 * (zi * b + y) + core).start()
+                hop(pb.at[d], pb.at[d], (fs_sem, z * b + y), (cr_sem, d), 2 * (zi * b + y) + core, d)("start")
 
             loop(1, b, to_y)
-            along_cells(pb.at[d], pb.at[d], ds_sem.at[t], cr_sem.at[d], sibling).start()
+            hop(pb.at[d], pb.at[d], (ds_sem, t), (cr_sem, d), sibling, d)("start")
 
         def arrived(d):
-            along_cells(pb.at[d], pb.at[d], ds_sem.at[0], cr_sem.at[d], sibling).wait_recv()
+            hop(pb.at[d], pb.at[d], (ds_sem, 0), (cr_sem, d), sibling, d)("wait_recv")
 
         def go(k):
             z = onward(k)
-            along_cells(pb.at[me], pb.at[me], cs_sem.at[z], cr_sem.at[me], 2 * (z * b + yi) + core).start()
-
+            hop(pb.at[me], pb.at[me], (cs_sem, z), (cr_sem, me), 2 * (z * b + yi) + core, me)("start")
+
+        seat = 2 * yi + core
+        late = max(a - 1, 1)
         if not final:
-            loop(1, min(2, a), go)
+            loop(1, a, go)
             relay(zi)
         phigh, pboth = keep(me, pb[me])
-        gz[zi] = product(phigh, pboth, vhi[me], vlo[me], ROWS)
-        spread(along_column, gz, zi, a, gzs_sem, gzr_sem)
+        gy[seat] = product(phigh, pboth, vhi[me], vlo[me], ROWS)
+        spread(along_plane, gy, seat, 2 * b, gys_sem, gyr_sem)
         if final:
-            loop(1, min(2, a), go)
             relay(zi)
-        loop(min(2, a), a, go)
-        if not final:
+            loop(1, late, go)
+        else:
             stack[pl.ds(position, BLOCK)] = (
                 pb[me] * (live_total * factor_scale) + tilt * stack[WEIGHT : WEIGHT + 1]
             )
@@ -578,6 +653,7 @@
             phigh, pboth = keep(d, pb[d])
             if final:
                 emit(d, pl.ds((STEPS - 1) * BLOCK, BLOCK), fresh(d))
+                shipped(d, "start")
             else:
                 xg[j + 1, mine] = xg[j + 1, mine] + product(phigh, pboth, lhi[d], llo[d], ROWS)
 
@@ -586,58 +662,19 @@
             arrived(2 * (z * b + yi) + core)
             relay(z)
 
-        seat = 2 * yi + core
         def quarter(q):
             if not final:
                 pl.when(j == 0)(lambda: loop(q * n // 4, (q + 1) * n // 4, meet))
 
-        quarter(0)
-        loop(1, min(2, a), pass_z)
-        quarter(1)
-        if not final:
-            loop(min(2, a), min(3, a), pass_z)
-        gx[mine] = gathered(along_column, gz, zi, a, gzs_sem, gzr_sem)
-        spread(along_genes, gx, mine, g, gxs_sem, gxr_sem)
-        if final:
-            loop(min(2, a), min(3, a), pass_z)
-        quarter(2)
-        loop(min(3, a), a, pass_z)
-        quarter(3)
-        if not final:
-            pl.when(j == 0)(lambda: spread(along_genes, xs0, mine, g, s0s_sem, s0r_sem))
-
-        def plane():
-            gy[seat] = gathered(along_genes, gx, mine, g, gxs_sem, gxr_sem)
-            spread(along_plane, gy, seat, 2 * b, gys_sem, gyr_sem)
-
-        def open_right():
-            met = gathered(along_genes, xs0, mine, g, s0s_sem, s0r_sem)
-            held = lax.broadcasted_iota(jnp.int32, met.shape, 1) < SLOTS
-            er[0 : BASIS + BLOCK] = jnp.where(held, met, 0.0)
-            r1[...], r2[...] = both_sides(er[...], same)
-
-        def close():
-            if not final:
-                pl.when(j == 0)(open_right)
-            total = gathered(along_plane, gy, seat, 2 * b, gys_sem, gyr_sem)
-            factor, against, change = orthonormal(total, r1[...], r2[...])
-            couple_out[j] = factor
-            chg[...] = change
-            if not final:
-                extend(er, r1, r2, position + BLOCK, against)
-
-        if final:
-            plane()
-            close()
-        consume(me)
-        loop(1, a, lambda k: consume(2 * (behind(k) * b + yi) + core))
+        def own(k):
+            consume(2 * (behind(k) * b + yi) + core)
 
         def pass_y(k):
             z = behind(lax.rem(k, a))
             t = z * b + lax.rem(yi + 1 + k // a, b)
             d = 2 * t + core
             arrived(d)
-            along_cells(pb.at[d], pb.at[d], ds_sem.at[t], cr_sem.at[d], sibling).start()
+            hop(pb.at[d], pb.at[d], (ds_sem, t), (cr_sem, d), sibling, d)("start")
             consume(d)
 
         def rest(k):
@@ -647,11 +684,72 @@
             arrived(d)
             consume(d)
 
+        def early(k):
+            if not final:
+                own(k)
+                rest(k - 1)
+
+        def ahead():
+            gx[mine] = gathered(along_plane, gy, seat, 2 * b, gys_sem, gyr_sem)
+            spread(along_genes, gx, mine, g, gxs_sem, gxr_sem)
+
+        if final:
+            ahead()
+        else:
+            consume(me)
+        quarter(0)
+        loop(1, min(2, a), pass_z)
         if not final:
-            plane()
-        loop(0, a, rest)
-        loop(0, h - a, pass_y)
-
+            ahead()
+        loop(1, min(2, a), early)
+        quarter(1)
+        if not final:
+            loop(min(2, a), min(3, a), pass_z)
+        gz[zi] = gathered(along_genes, gx, mine, g, gxs_sem, gxr_sem)
+        spread(along_column, gz, zi, a, gzs_sem, gzr_sem)
+        if final:
+            loop(late, a, go)
+            loop(min(2, a), min(3, a), pass_z)
+        loop(min(2, a), min(3, a), early)
+        met = min(1, h - a)
+        if not final:
+            loop(0, met, pass_y)
+        quarter(2)
+
+        def follow(k):
+            pass_z(k)
+            early(k)
+
+        loop(min(3, a), a, follow)
+        quarter(3)
+        if not final:
+            pl.when(j == 0)(lambda: spread(along_genes, xs0, mine, g, s0s_sem, s0r_sem))
+
+        def open_right():
+            met = gathered(along_genes, xs0, mine, g, s0s_sem, s0r_sem)
+            held = lax.broadcasted_iota(jnp.int32, met.shape, 1) < SLOTS
+            er[0 : BASIS + BLOCK] = jnp.where(held, met, 0.0)
+            r1[...], r2[...] = both_sides(er[...], same)
+
+        def close():
+            if not final:
+                pl.when(j == 0)(open_right)
+            total = gathered(along_column, gz, zi, a, gzs_sem, gzr_sem)
+            factor, against, change = orthonormal(total, r1[...], r2[...])
+            couple_out[j] = factor
+            chg[...] = change
+            if not final:
+                extend(er, r1, r2, position + BLOCK, against)
+
+        if final:
+            close()
+            consume(me)
+            loop(1, a, own)
+            loop(0, a, rest)
+            loop(0, h - a, pass_y)
+        else:
+            rest(a - 1)
+            loop(met, h - a, pass_y)
         loop(a, h, rest)
         if not final:
             spread(along_genes, xg.at[j + 1], mine, g, xs_sem.at[j + 1], xr_sem.at[j + 1])
@@ -659,26 +757,44 @@
         walk.ended()
 
         def ended(t):
-            along_cells(pb.at[t], pb.at[t], ds_sem.at[t], cr_sem.at[t], sibling).wait_send()
+            hop(pb.at[t], pb.at[t], (ds_sem, t), (cr_sem, t), sibling, 2 * t + core)("wait_send")
 
         loop(0, h, ended)
 
         def ended_y(k):
             z, y = order(k)
             t = z * b + y
-            along_cells(pb.at[t], pb.at[t], fs_sem.at[t], cr_sem.at[t], sibling).wait_send()
+            hop(pb.at[t], pb.at[t], (fs_sem, t), (cr_sem, t), sibling, 2 * (z * b + yi) + core)("wait_send")
 
         loop(0, h - a, ended_y)
 
         def ended_z(k):
             z = lax.rem(zi + k, a)
-            along_cells(pb.at[z], pb.at[z], cs_sem.at[z], cr_sem.at[z], sibling).wait_send()
+            hop(pb.at[z], pb.at[z], (cs_sem, z), (cr_sem, z), sibling, me)("wait_send")
 
         loop(1, a, ended_z)
 
     loop(0, STEPS - 1, lambda j: step(j, False))
     step(STEPS - 1, True)
     base.ended()
+    loop(0, n, lambda d: shipped(d, "wait"))
+    loop(0, STEPS - 1, lambda j: block(j).wait())
+
+
+def settle_outputs(left, right, diag, couple, left_out, right_out, diag_out, couple_out, lv, rv, dv, cv, came, went):
+    routes = [(left, lv, left_out), (diag, dv, diag_out), (couple, cv, couple_out)]
+    for i in range(right.shape[0] // 8):
+        rows = pl.ds(i * 8, 8)
+        routes.append((right.at[rows], rv.at[rows], right_out.at[rows]))
+    fetch = [pltpu.make_async_copy(src, mid, came.at[i]) for i, (src, mid, _) in enumerate(routes)]
+    store = [pltpu.make_async_copy(mid, dst, went.at[i]) for i, (_, mid, dst) in enumerate(routes)]
+    for item in fetch:
+        item.start()
+    for item, onward in zip(fetch, store):
+        item.wait()
+        onward.start()
+    for item in store:
+        item.wait()
 
 
 def body(counts, live_rows, left_basis, right_basis, right_start):
@@ -686,7 +802,8 @@
     n = lax.axis_size("cells")
     g = lax.axis_size("genes")
     h = n // 2
-    width = -(-(genes // LANES) // n) * LANES
+    brief, longs = chunks(n, genes)
+    width = (brief + (1 if longs else 0)) * LANES
     scales = (math.sqrt(float(cells * n)), math.sqrt(float(genes * g)))
     vmem = pl.BlockSpec(memory_space=pltpu.VMEM)
     anywhere = pl.BlockSpec(memory_space=pl.ANY)
@@ -703,6 +820,7 @@
         held(n, rows, width), held(h, rows, width), held(h, rows, width), held(h, rows, width),
     ]
     scratch = [
+        held(STEPS * BLOCK, genes),
         pltpu.VMEM((n, cells, width), jnp.int32),
         held(n, cells, width),
         *[pltpu.VMEM((n, cells, width), BF16)] * 2,
@@ -727,25 +845,32 @@
         held(g, BLOCK, LANES),
         held(n, BLOCK, LANES),
         held(h, BLOCK, LANES),
-        dma(n, 3),
-        *[dma(h)] * 6,
-        *[dma(h)] * 6,
-        dma(h), dma(n), dma(h), dma(h), dma(n), dma(n),
+        dma(n, 3, 2),
+        *[dma(2, h)] * 12,
+        dma(2, h), dma(2, n), dma(2, h), dma(2, h), dma(n), dma(n),
         *[dma(n)] * 6,
         *[dma(g)] * 4,
         dma(STEPS, g), dma(STEPS, g),
-        dma(g), dma(g), dma(n), dma(n), dma(h), dma(h),
+        dma(g), dma(g), dma(n), dma(n), dma(h), dma(h), dma(STEPS), dma(n, 2),
     ]
-    return pl.pallas_call(
+    results = pl.pallas_call(
         functools.partial(kernel, n, g, width, scales),
         out_shape=out_shape,
         in_specs=[pl.BlockSpec(memory_space=pltpu.SMEM), anywhere, vmem, anywhere, anywhere],
-        out_specs=(vmem, vmem, vmem, vmem),
+        out_specs=(vmem, anywhere, vmem, vmem),
         scratch_shapes=scratch,
         compiler_params=pltpu.CompilerParams(
             collective_id=0, has_side_effects=True, vmem_limit_bytes=66 * 1000 * 1000
         ),
     )(live_rows, counts, left_basis, right_basis, right_start)
+    moves = 3 + STEPS * BLOCK // 8
+    return pl.pallas_call(
+        settle_outputs,
+        out_shape=out_shape,
+        in_specs=[anywhere] * 4,
+        out_specs=(anywhere,) * 4,
+        scratch_shapes=[pltpu.VMEM(item.shape, F32) for item in out_shape] + [dma(moves), dma(moves)],
+    )(*results)
 
 
 def solution(mesh):

time: 145 us -> 133 us (0.917)
  local copies, waits for them, and re-layouts: 6.37 us -> 0 us
  Pallas kernels: 137 us -> 132 us
    pallas_call x1, Pallas kernels: 137 us -> 129 us  [body(): pl.pallas_call(functools.partial(kernel, n, g, width, scales), out_shape=...]
    unnamed x8 -> x0, local copies, waits for them, and re-layouts: 6.37 us -> none
    pallas_call x0 -> x1, Pallas kernels: none -> 2.93 us  [body(): pl.pallas_call(settle_outputs, out_shape=out_shape, in_specs=[anywhere] *...]
where the time goes in v4:
time: 133 us
  Pallas kernels  132 us (99%)
    pallas_call x1, Pallas kernels, body(): pl.pallas_call(functools.partial(kernel, n, g, width, scales), out_shape=...  129 us
    pallas_call x1, Pallas kernels, body(): pl.pallas_call(settle_outputs, out_shape=out_shape, in_specs=[anywhere] *...  2.93 us

profile of v4, /device:TPU:0, one launch (start us, length us, event | category | flops | bytes accessed | tf_op | source)
XLA Modules:
  0.0 132.9 jit_solution(12973946879404427896)
XLA Ops:
  1.3 128.7 %shard_map.84 = (f32[48,128]{1,0:T(8,128)}, f32[48,16640]{1,0:T(8,128)}, f32[3,16,16]{2,1,0:T(8,128)}, f32[3,16,16]{2,1,0:T(8,128)}) custom-call(s32[1]{0:T(128)S(6)} %copy.9.live, s32[128,16640]{1,0:T(8,128)} %counts.1, f32[32,128]{1,0:T(8,128)} %left_basis.1, f32[32,16640]{1,0:T(8,128)} %right_basis.1, f32[16,16640]{1,0:T(8,128)} %right_start.1), custom_call_target="tpu_custom_call" | custom-call | tf_op jit(solution)/shard_map/pallas_call | solution.py:856
  130.0 2.9 %shard_map.85 = (f32[48,128]{1,0:T(8,128)}, f32[48,16640]{1,0:T(8,128)}, f32[3,16,16]{2,1,0:T(8,128)}, f32[3,16,16]{2,1,0:T(8,128)}) custom-call(f32[48,128]{1,0:T(8,128)} %get-tuple-element.8.left, f32[48,16640]{1,0:T(8,128)} %get-tuple-element.9.right, f32[3,16,16]{2,1,0:T(8,128)} %get-tuple-element.10.diag, f32[3,16,16]{2,1,0:T(8,128)} %get-tuple-element.11.couple), custom_call_target="tpu_custom_call" | custom-call | tf_op jit(solution)/shard_map/pallas_call | solution.py:867

commit v5 on v4

--- a/solution.py
+++ b/solution.py
@@ -88,6 +88,12 @@
     return factor[:, :BLOCK], residue, change
 
 
+def grid(h):
+    b = 1 << ((h.bit_length() - 1) // 2)
+    b = b if h % b == 0 else 1
+    return h // b, b
+
+
 def chunks(n, genes):
     brief, extra = divmod(genes // LANES, n)
     stride = n // extra if extra else n
@@ -100,11 +106,11 @@
     left_out, right_hbm, diag_out, couple_out,
     right_out, cnt, logged, lhi, llo, vhi, vlo, rb, sl, mr, el, er, l1, l2, r1, r2,
     w, ra, rt, rz, wb, rab, rtb, rzb, pb, stack, ground, tpart, tfrom,
-    mu, wsum, chg, gram0, gram, xs0, xb0, xg, gx, gy, gz,
+    mu, wsum, chg, gram0, gramz, gram, gramc, xs0, xb0, xg, gx, gy, gz,
     in_sem, as_sem, ar_sem, bs_sem, br_sem, zs_sem, zr_sem,
     bas_sem, bar_sem, bbs_sem, bbr_sem, bzs_sem, bzr_sem,
     cs_sem, cr_sem, ds_sem, fs_sem, ts_sem, tr_sem,
-    ms_sem, mr_sem, g0s_sem, g0r_sem, gs_sem, gr_sem, s0s_sem, s0r_sem, b0s_sem, b0r_sem,
+    ms_sem, mr_sem, g0s_sem, g0r_sem, g0zs_sem, g0zr_sem, gs_sem, gr_sem, gcs_sem, gcr_sem, s0s_sem, s0r_sem, b0s_sem, b0r_sem,
     xs_sem, xr_sem, gxs_sem, gxr_sem, gys_sem, gyr_sem, gzs_sem, gzr_sem, out_sem, tail_sem,
 ):
     cells, genes = counts.shape
@@ -113,11 +119,10 @@
     core = lax.rem(me, 2)
     chip = me // 2
     h = n // 2
-    b = 1 << ((h.bit_length() - 1) // 2)
-    b = b if h % b == 0 else 1
-    a = h // b
+    a, b = grid(h)
     zi, yi = chip // b, lax.rem(chip, b)
     sibling = me + 1 - 2 * core
+    seat = 2 * yi + core
     tiles = width // LANES
     brief, longs = chunks(n, genes)
     brief = brief * LANES
@@ -370,23 +375,23 @@
     sl[WEIGHT : WEIGHT + 8] = jnp.where(
         lax.broadcasted_iota(jnp.int32, (8, cells), 0) == 0, weights_row, 0.0
     )
-    gram0[me, 0:BASIS] = exact_rows(sl[0:BASIS], sl[...])
-    gram0[me, BASIS:] = exact_rows(sl[WEIGHT : WEIGHT + 8], sl[...])
+    gram0[seat, 0:BASIS] = exact_rows(sl[0:BASIS], sl[...])
+    gram0[seat, BASIS:] = exact_rows(sl[WEIGHT : WEIGHT + 8], sl[...])
 
     def take_log(d):
         for i in range(tiles):
             here = slice(i * LANES, (i + 1) * LANES)
-            logged[d, :, here] = jnp.log(1.0 + cnt[d, :, here].astype(F32)) * weights
+            logged[d, :, here] = jnp.log(1.0 + cnt[d, :, here].astype(F32))
 
     fill_in(me, 0, "wait")
     take_log(me)
     portion = 1.0 / jnp.maximum(live_here, 1).astype(F32)
     for i in range(tiles):
         here = slice(i * LANES, (i + 1) * LANES)
-        mu[me, :, here] = jnp.sum(logged[me, :, here], axis=0, keepdims=True) * portion
+        mu[me, :, here] = jnp.sum(logged[me, :, here] * weights, axis=0, keepdims=True) * portion
     pl.semaphore_wait(barrier, n - 1 + g - 1)
     spread(along_cells, mu, me, n, ms_sem, mr_sem)
-    spread(along_cells, gram0, me, n, g0s_sem, g0r_sem)
+    spread(along_plane, gram0, seat, 2 * b, g0s_sem, g0r_sem)
 
     def next_log(k):
         fill_in(around(k), 0, "wait")
@@ -409,6 +414,14 @@
         vlo[d, BASIS + BLOCK :] = blank
 
     loop(0, n, fill)
+    def meet(d):
+        high = vhi[d, 0 : BASIS + BLOCK]
+        both = jnp.concatenate([high, vlo[d, 0 : BASIS + BLOCK]], axis=0)
+        xs0[mine] = xs0[mine] + product(high, both, vhi[d], vlo[d], ROWS)
+
+    loop(0, n // 2, meet, 2)
+    gramz[zi] = gathered(along_plane, gram0, seat, 2 * b, g0s_sem, g0r_sem)
+    spread(along_column, gramz, zi, a, g0zs_sem, g0zr_sem)
     waited(along_cells, mu, me, n, ms_sem, mr_sem)
 
     bhigh, blow = split(jnp.concatenate(
@@ -419,7 +432,7 @@
     def center(d):
         for i in range(tiles):
             here = slice(i * LANES, (i + 1) * LANES)
-            high, low = split(logged[d, :, here] - weights * mu[d, :, here])
+            high, low = split(logged[d, :, here] - mu[d, :, here])
             lhi[d, :, here] = high
             llo[d, :, here] = low
         made = product(bhigh, bboth, lhi[d], llo[d], ALONG)
@@ -441,13 +454,14 @@
         xb0[mine] = xb0[mine] + met[0:BASIS]
         xg[0, mine] = xg[0, mine] + met[BASIS:]
 
+    loop(0, n // 2, cross, 2)
     base.third(0, 1)
-    loop(0, n, cross, 2)
+    loop(n // 2, n, cross, 2)
     spread(along_genes, xg.at[0], mine, g, xs_sem.at[0], xr_sem.at[0])
     spread(along_genes, xb0, mine, g, b0s_sem, b0r_sem)
     base.third(1, 2)
 
-    near = gathered(along_cells, gram0, me, n, g0s_sem, g0r_sem)
+    near = gathered(along_column, gramz, zi, a, g0zs_sem, g0zr_sem)
     corner = lax.broadcasted_iota(jnp.int32, (LANES, LANES), 0)
     across = lax.broadcasted_iota(jnp.int32, (BASIS, LANES), 1)
     el[...] = jnp.where((same > 0) & (corner >= BASIS), 1.0, 0.0)
@@ -513,11 +527,6 @@
         vlo[d, SLOTS : SLOTS + BLOCK] = plow
         return phigh, jnp.concatenate([phigh, plow], axis=0)
 
-    def meet(d):
-        high = vhi[d, 0 : BASIS + BLOCK]
-        both = jnp.concatenate([high, vlo[d, 0 : BASIS + BLOCK]], axis=0)
-        xs0[mine] = xs0[mine] + product(high, both, vhi[d], vlo[d], ROWS)
-
     def begin(j):
         @pl.when(j == 0)
         def _():
@@ -527,12 +536,12 @@
     def step(j, final):
         position = BASIS + j * BLOCK
         position = position if final else pl.multiple_of(position, BLOCK)
-        mr[SLOTS : SLOTS + BLOCK] = gathered(along_genes, xg.at[j], mine, g, xs_sem.at[j], xr_sem.at[j])
+        mr[SLOTS : SLOTS + BLOCK] = gathered(along_genes, xg.at[j], mine, g, xs_sem.at[j], xr_sem.at[j]) * weights_row
         vectors = exact(chg[...], mr[...])
         mr[pl.ds(position, BLOCK)] = vectors
         sl[SLOTS : SLOTS + BLOCK] = vectors
-        gram[me] = exact_rows(vectors, sl[...])
-        spread(along_cells, gram, me, n, gs_sem, gr_sem)
+        gram[seat] = exact_rows(vectors, sl[...])
+        spread(along_plane, gram, seat, 2 * b, gs_sem, gr_sem)
         high, low = split(vectors)
         both = jnp.concatenate([high, low], axis=0)
 
@@ -540,24 +549,28 @@
             w[d] = product(high, both, lhi[d], llo[d], ALONG)
 
         walk.launch(produce)
+        gramc[zi] = gathered(along_plane, gram, seat, 2 * b, gs_sem, gr_sem)
+        spread(along_column, gramc, zi, a, gcs_sem, gcr_sem)
         if final:
-            update(j - 1, 0, n // 2)
+            update(j - 1, 0, n // 4)
             walk.third(0, 1)
+            update(j - 1, n // 4, n // 2)
+            walk.third(1, 2)
             update(j - 1, n // 2, n)
             block(j - 1).start()
-            walk.third(1, 2)
         else:
             begin(j)
 
             @pl.when(j > 0)
             def _():
-                update(j - 1, 0, n // 2)
+                update(j - 1, 0, n // 4)
                 walk.third(0, 1)
+                update(j - 1, n // 4, n // 2)
+                walk.third(1, 2)
                 update(j - 1, n // 2, n)
                 block(j - 1).start()
-                walk.third(1, 2)
-
-        total = gathered(along_cells, gram, me, n, gs_sem, gr_sem)
+
+        total = gathered(along_column, gramc, zi, a, gcs_sem, gcr_sem)
         held = total[:, WEIGHT : WEIGHT + 1] * inverse
         weighed = wsum[0:1] + turned(total[:, WEIGHT : WEIGHT + 1], SLOTS)
         scale = jnp.where(lane < SLOTS, factor_scale, factor_scale * factor_scale)
@@ -602,7 +615,7 @@
                 loop(1, n, take)
                 stack[WEIGHT : WEIGHT + 1] = tpart[me]
                 settle()
-                mr[0:BASIS] = gathered(along_genes, xb0, mine, g, b0s_sem, b0r_sem)
+                mr[0:BASIS] = gathered(along_genes, xb0, mine, g, b0s_sem, b0r_sem) * weights_row
 
         walk.fourth(stack, slice(SLOTS, SLOTS + BLOCK))
         columns = [blend[:, SLOTS + k : SLOTS + k + 1] for k in range(BLOCK)]
@@ -631,17 +644,25 @@
             z = onward(k)
             hop(pb.at[me], pb.at[me], (cs_sem, z), (cr_sem, me), 2 * (z * b + yi) + core, me)("start")
 
-        seat = 2 * yi + core
-        late = max(a - 1, 1)
         if not final:
             loop(1, a, go)
             relay(zi)
         phigh, pboth = keep(me, pb[me])
-        gy[seat] = product(phigh, pboth, vhi[me], vlo[me], ROWS)
-        spread(along_plane, gy, seat, 2 * b, gys_sem, gyr_sem)
+        square = product(phigh, pboth, vhi[me], vlo[me], ROWS)
+        plane = (along_plane, gy, seat, 2 * b, gys_sem, gyr_sem)
+        line = (along_genes, gx, mine, g, gxs_sem, gxr_sem)
+        column = (along_column, gz, zi, a, gzs_sem, gzr_sem)
+        stages = (column, line, plane) if final else (plane, line, column)
+
+        def advance(i):
+            copy, buf, at = stages[i][:3]
+            buf[at] = gathered(*stages[i - 1]) if i else square
+            spread(*stages[i])
+
+        advance(0)
         if final:
             relay(zi)
-            loop(1, late, go)
+            loop(1, a, go)
         else:
             stack[pl.ds(position, BLOCK)] = (
                 pb[me] * (live_total * factor_scale) + tilt * stack[WEIGHT : WEIGHT + 1]
@@ -664,7 +685,7 @@
 
         def quarter(q):
             if not final:
-                pl.when(j == 0)(lambda: loop(q * n // 4, (q + 1) * n // 4, meet))
+                pl.when(j == 0)(lambda: loop(n // 2 + q * n // 8, n // 2 + (q + 1) * n // 8, meet))
 
         def own(k):
             consume(2 * (behind(k) * b + yi) + core)
@@ -689,40 +710,30 @@
                 own(k)
                 rest(k - 1)
 
-        def ahead():
-            gx[mine] = gathered(along_plane, gy, seat, 2 * b, gys_sem, gyr_sem)
-            spread(along_genes, gx, mine, g, gxs_sem, gxr_sem)
-
-        if final:
-            ahead()
-        else:
-            consume(me)
-        quarter(0)
-        loop(1, min(2, a), pass_z)
-        if not final:
-            ahead()
-        loop(1, min(2, a), early)
-        quarter(1)
-        if not final:
-            loop(min(2, a), min(3, a), pass_z)
-        gz[zi] = gathered(along_genes, gx, mine, g, gxs_sem, gxr_sem)
-        spread(along_column, gz, zi, a, gzs_sem, gzr_sem)
-        if final:
-            loop(late, a, go)
-            loop(min(2, a), min(3, a), pass_z)
-        loop(min(2, a), min(3, a), early)
-        met = min(1, h - a)
-        if not final:
-            loop(0, met, pass_y)
-        quarter(2)
-
         def follow(k):
             pass_z(k)
             early(k)
 
-        loop(min(3, a), a, follow)
-        quarter(3)
-        if not final:
+        met = min(1, h - a)
+        if final:
+            advance(1)
+            loop(1, min(2, a), pass_z)
+            advance(2)
+            loop(min(2, a), a, pass_z)
+        else:
+            consume(me)
+            quarter(0)
+            loop(1, min(2, a), pass_z)
+            loop(1, min(2, a), early)
+            advance(1)
+            quarter(1)
+            loop(min(2, a), min(3, a), pass_z)
+            loop(min(2, a), min(3, a), early)
+            loop(0, met, pass_y)
+            advance(2)
+            quarter(2)
+            loop(min(3, a), a, follow)
+            quarter(3)
             pl.when(j == 0)(lambda: spread(along_genes, xs0, mine, g, s0s_sem, s0r_sem))
 
         def open_right():
@@ -734,7 +745,7 @@
         def close():
             if not final:
                 pl.when(j == 0)(open_right)
-            total = gathered(along_column, gz, zi, a, gzs_sem, gzr_sem)
+            total = gathered(*stages[2])
             factor, against, change = orthonormal(total, r1[...], r2[...])
             couple_out[j] = factor
             chg[...] = change
@@ -802,6 +813,7 @@
     n = lax.axis_size("cells")
     g = lax.axis_size("genes")
     h = n // 2
+    a, b = grid(h)
     brief, longs = chunks(n, genes)
     width = (brief + (1 if longs else 0)) * LANES
     scales = (math.sqrt(float(cells * n)), math.sqrt(float(genes * g)))
@@ -837,21 +849,24 @@
         held(n, 1, width),
         held(8, LANES),
         held(BLOCK, LANES),
-        held(n, BASIS + 8, LANES),
-        held(n, BLOCK, LANES),
+        held(2 * b, BASIS + 8, LANES),
+        held(a, BASIS + 8, LANES),
+        held(2 * b, BLOCK, LANES),
+        held(a, BLOCK, LANES),
         held(g, BASIS + BLOCK, LANES),
         held(g, BASIS, LANES),
         held(STEPS, g, BLOCK, LANES),
         held(g, BLOCK, LANES),
-        held(n, BLOCK, LANES),
-        held(h, BLOCK, LANES),
+        held(2 * b, BLOCK, LANES),
+        held(a, BLOCK, LANES),
         dma(n, 3, 2),
         *[dma(2, h)] * 12,
         dma(2, h), dma(2, n), dma(2, h), dma(2, h), dma(n), dma(n),
-        *[dma(n)] * 6,
+        dma(n), dma(n),
+        *[dma(2 * b), dma(2 * b), dma(a), dma(a)] * 2,
         *[dma(g)] * 4,
         dma(STEPS, g), dma(STEPS, g),
-        dma(g), dma(g), dma(n), dma(n), dma(h), dma(h), dma(STEPS), dma(n, 2),
+        dma(g), dma(g), dma(2 * b), dma(2 * b), dma(a), dma(a), dma(STEPS), dma(n, 2),
     ]
     results = pl.pallas_call(
         functools.partial(kernel, n, g, width, scales),

time: 133 us -> 128 us (0.962)
  Pallas kernels: 132 us -> 126 us
    pallas_call x1, Pallas kernels: 129 us -> 123 us  [body(): pl.pallas_call(functools.partial(kernel, n, g, width, scales), out_shape=...]
where the time goes in v5:
time: 128 us; the launch traced here: 127 us
  Pallas kernels  126 us (98%)
  between operations  1.28 us (1%)
    pallas_call x1, Pallas kernels, body(): pl.pallas_call(functools.partial(kernel, n, g, width, scales), out_shape=...  123 us
    pallas_call x1, Pallas kernels, body(): pl.pallas_call(settle_outputs, out_shape=out_shape, in_specs=[anywhere] *...  2.93 us

profile of v5, /device:TPU:0, one launch (start us, length us, event | category | flops | bytes accessed | tf_op | source)
XLA Modules:
  0.0 127.1 jit_solution(3880533416584523663)
XLA Ops:
  1.3 122.9 %shard_map.84 = (f32[48,128]{1,0:T(8,128)}, f32[48,16640]{1,0:T(8,128)}, f32[3,16,16]{2,1,0:T(8,128)}, f32[3,16,16]{2,1,0:T(8,128)}) custom-call(s32[1]{0:T(128)S(6)} %copy.9.live, s32[128,16640]{1,0:T(8,128)} %counts.1, f32[32,128]{1,0:T(8,128)} %left_basis.1, f32[32,16640]{1,0:T(8,128)} %right_basis.1, f32[16,16640]{1,0:T(8,128)} %right_start.1), custom_call_target="tpu_custom_call" | custom-call | tf_op jit(solution)/shard_map/pallas_call | solution.py:871
  124.2 2.9 %shard_map.85 = (f32[48,128]{1,0:T(8,128)}, f32[48,16640]{1,0:T(8,128)}, f32[3,16,16]{2,1,0:T(8,128)}, f32[3,16,16]{2,1,0:T(8,128)}) custom-call(f32[48,128]{1,0:T(8,128)} %get-tuple-element.8.left, f32[48,16640]{1,0:T(8,128)} %get-tuple-element.9.right, f32[3,16,16]{2,1,0:T(8,128)} %get-tuple-element.10.diag, f32[3,16,16]{2,1,0:T(8,128)} %get-tuple-element.11.couple), custom_call_target="tpu_custom_call" | custom-call | tf_op jit(solution)/shard_map/pallas_call | solution.py:882

commit v6 on v5

--- a/solution.py
+++ b/solution.py
@@ -103,15 +103,15 @@
 def kernel(
     n, g, width, scales,
     live, counts, left_basis, right_basis, right_start,
-    left_out, right_hbm, diag_out, couple_out,
-    right_out, cnt, logged, lhi, llo, vhi, vlo, rb, sl, mr, el, er, l1, l2, r1, r2,
+    left_out, right_out, diag_out, couple_out,
+    cnt, logged, lhi, llo, vhi, vlo, rb, sl, mr, el, er, l1, l2, r1, r2,
     w, ra, rt, rz, wb, rab, rtb, rzb, pb, stack, ground, tpart, tfrom,
     mu, wsum, chg, gram0, gramz, gram, gramc, xs0, xb0, xg, gx, gy, gz,
     in_sem, as_sem, ar_sem, bs_sem, br_sem, zs_sem, zr_sem,
     bas_sem, bar_sem, bbs_sem, bbr_sem, bzs_sem, bzr_sem,
     cs_sem, cr_sem, ds_sem, fs_sem, ts_sem, tr_sem,
     ms_sem, mr_sem, g0s_sem, g0r_sem, g0zs_sem, g0zr_sem, gs_sem, gr_sem, gcs_sem, gcr_sem, s0s_sem, s0r_sem, b0s_sem, b0r_sem,
-    xs_sem, xr_sem, gxs_sem, gxr_sem, gys_sem, gyr_sem, gzs_sem, gzr_sem, out_sem, tail_sem,
+    xs_sem, xr_sem, gxs_sem, gxr_sem, gys_sem, gyr_sem, gzs_sem, gzr_sem,
 ):
     cells, genes = counts.shape
     me = lax.axis_index("cells")
@@ -389,15 +389,15 @@
     for i in range(tiles):
         here = slice(i * LANES, (i + 1) * LANES)
         mu[me, :, here] = jnp.sum(logged[me, :, here] * weights, axis=0, keepdims=True) * portion
+    def next_log(k):
+        fill_in(around(k), 0, "wait")
+        take_log(around(k))
+
+    loop(1, n, next_log)
     pl.semaphore_wait(barrier, n - 1 + g - 1)
     spread(along_cells, mu, me, n, ms_sem, mr_sem)
     spread(along_plane, gram0, seat, 2 * b, g0s_sem, g0r_sem)
 
-    def next_log(k):
-        fill_in(around(k), 0, "wait")
-        take_log(around(k))
-
-    loop(1, n, next_log)
     xs0[mine] = jnp.zeros((BASIS + BLOCK, LANES), F32)
     xb0[mine] = jnp.zeros((BASIS, LANES), F32)
     xg[0, mine] = jnp.zeros((BLOCK, LANES), F32)
@@ -461,6 +461,8 @@
     spread(along_genes, xb0, mine, g, b0s_sem, b0r_sem)
     base.third(1, 2)
 
+    loop(n // 2, n, meet, 2)
+    spread(along_genes, xs0, mine, g, s0s_sem, s0r_sem)
     near = gathered(along_column, gramz, zi, a, g0zs_sem, g0zr_sem)
     corner = lax.broadcasted_iota(jnp.int32, (LANES, LANES), 0)
     across = lax.broadcasted_iota(jnp.int32, (BASIS, LANES), 1)
@@ -490,24 +492,6 @@
             def _():
                 right_out[rows, pl.ds(pl.multiple_of(at + brief, LANES), LANES)] = values[:, brief:]
 
-    def shipped(d, method):
-        rows = pl.ds((STEPS - 1) * BLOCK, BLOCK)
-        at = first_gene(d)
-
-        def act(start, size, which):
-            here = pl.ds(start, size)
-            getattr(pltpu.make_async_copy(
-                right_out.at[rows, here], right_hbm.at[rows, here], tail_sem.at[d, which]
-            ), method)()
-
-        act(at, brief, 0)
-        if longs:
-            pl.when(is_long(d))(lambda: act(pl.multiple_of(at + brief, LANES), LANES, 1))
-
-    def block(j):
-        rows = pl.ds(j * BLOCK if isinstance(j, int) else pl.multiple_of(j * BLOCK, BLOCK), BLOCK)
-        return pltpu.make_async_copy(right_out.at[rows], right_hbm.at[rows], out_sem.at[j])
-
     def update(j, start, stop):
         later = pl.multiple_of(BASIS + (j + 1) * BLOCK, BLOCK)
         rows = pl.ds(pl.multiple_of(j * BLOCK, BLOCK), BLOCK)
@@ -557,7 +541,6 @@
             update(j - 1, n // 4, n // 2)
             walk.third(1, 2)
             update(j - 1, n // 2, n)
-            block(j - 1).start()
         else:
             begin(j)
 
@@ -568,7 +551,6 @@
                 update(j - 1, n // 4, n // 2)
                 walk.third(1, 2)
                 update(j - 1, n // 2, n)
-                block(j - 1).start()
 
         total = gathered(along_column, gramc, zi, a, gcs_sem, gcr_sem)
         held = total[:, WEIGHT : WEIGHT + 1] * inverse
@@ -617,8 +599,8 @@
                 settle()
                 mr[0:BASIS] = gathered(along_genes, xb0, mine, g, b0s_sem, b0r_sem) * weights_row
 
+        columns = [jnp.broadcast_to(blend[:, SLOTS + k : SLOTS + k + 1], (BLOCK, LANES)) for k in range(BLOCK)]
         walk.fourth(stack, slice(SLOTS, SLOTS + BLOCK))
-        columns = [blend[:, SLOTS + k : SLOTS + k + 1] for k in range(BLOCK)]
         for i in range(tiles):
             here = slice(i * LANES, (i + 1) * LANES)
             values = ground[:, here]
@@ -674,7 +656,6 @@
             phigh, pboth = keep(d, pb[d])
             if final:
                 emit(d, pl.ds((STEPS - 1) * BLOCK, BLOCK), fresh(d))
-                shipped(d, "start")
             else:
                 xg[j + 1, mine] = xg[j + 1, mine] + product(phigh, pboth, lhi[d], llo[d], ROWS)
 
@@ -682,10 +663,6 @@
             z = behind(k)
             arrived(2 * (z * b + yi) + core)
             relay(z)
-
-        def quarter(q):
-            if not final:
-                pl.when(j == 0)(lambda: loop(n // 2 + q * n // 8, n // 2 + (q + 1) * n // 8, meet))
 
         def own(k):
             consume(2 * (behind(k) * b + yi) + core)
@@ -722,19 +699,14 @@
             loop(min(2, a), a, pass_z)
         else:
             consume(me)
-            quarter(0)
             loop(1, min(2, a), pass_z)
             loop(1, min(2, a), early)
             advance(1)
-            quarter(1)
             loop(min(2, a), min(3, a), pass_z)
             loop(min(2, a), min(3, a), early)
             loop(0, met, pass_y)
             advance(2)
-            quarter(2)
             loop(min(3, a), a, follow)
-            quarter(3)
-            pl.when(j == 0)(lambda: spread(along_genes, xs0, mine, g, s0s_sem, s0r_sem))
 
         def open_right():
             met = gathered(along_genes, xs0, mine, g, s0s_sem, s0r_sem)
@@ -788,23 +760,18 @@
     loop(0, STEPS - 1, lambda j: step(j, False))
     step(STEPS - 1, True)
     base.ended()
-    loop(0, n, lambda d: shipped(d, "wait"))
-    loop(0, STEPS - 1, lambda j: block(j).wait())
-
-
-def settle_outputs(left, right, diag, couple, left_out, right_out, diag_out, couple_out, lv, rv, dv, cv, came, went):
-    routes = [(left, lv, left_out), (diag, dv, diag_out), (couple, cv, couple_out)]
-    for i in range(right.shape[0] // 8):
-        rows = pl.ds(i * 8, 8)
-        routes.append((right.at[rows], rv.at[rows], right_out.at[rows]))
-    fetch = [pltpu.make_async_copy(src, mid, came.at[i]) for i, (src, mid, _) in enumerate(routes)]
-    store = [pltpu.make_async_copy(mid, dst, went.at[i]) for i, (_, mid, dst) in enumerate(routes)]
-    for item in fetch:
+
+
+def settle_outputs(left, right, diag, couple, left_out, right_out, diag_out, couple_out, went):
+    items = [
+        pltpu.make_async_copy(src, dst, went.at[i])
+        for i, (src, dst) in enumerate(
+            [(right, right_out), (left, left_out), (diag, diag_out), (couple, couple_out)]
+        )
+    ]
+    for item in items:
         item.start()
-    for item, onward in zip(fetch, store):
-        item.wait()
-        onward.start()
-    for item in store:
+    for item in items:
         item.wait()
 
 
@@ -832,7 +799,6 @@
         held(n, rows, width), held(h, rows, width), held(h, rows, width), held(h, rows, width),
     ]
     scratch = [
-        held(STEPS * BLOCK, genes),
         pltpu.VMEM((n, cells, width), jnp.int32),
         held(n, cells, width),
         *[pltpu.VMEM((n, cells, width), BF16)] * 2,
@@ -866,26 +832,25 @@
         *[dma(2 * b), dma(2 * b), dma(a), dma(a)] * 2,
         *[dma(g)] * 4,
         dma(STEPS, g), dma(STEPS, g),
-        dma(g), dma(g), dma(2 * b), dma(2 * b), dma(a), dma(a), dma(STEPS), dma(n, 2),
+        dma(g), dma(g), dma(2 * b), dma(2 * b), dma(a), dma(a),
     ]
     results = pl.pallas_call(
         functools.partial(kernel, n, g, width, scales),
-        out_shape=out_shape,
+        out_shape=tuple(pltpu.VMEM(item.shape, F32) for item in out_shape),
         in_specs=[pl.BlockSpec(memory_space=pltpu.SMEM), anywhere, vmem, anywhere, anywhere],
-        out_specs=(vmem, anywhere, vmem, vmem),
+        out_specs=(vmem, vmem, vmem, vmem),
         scratch_shapes=scratch,
         compiler_params=pltpu.CompilerParams(
-            collective_id=0, has_side_effects=True, vmem_limit_bytes=66 * 1000 * 1000
+            collective_id=0, has_side_effects=True, vmem_limit_bytes=60 * 1000 * 1000
         ),
     )(live_rows, counts, left_basis, right_basis, right_start)
-    moves = 3 + STEPS * BLOCK // 8
     return pl.pallas_call(
         settle_outputs,
         out_shape=out_shape,
-        in_specs=[anywhere] * 4,
+        in_specs=[vmem] * 4,
         out_specs=(anywhere,) * 4,
-        scratch_shapes=[pltpu.VMEM(item.shape, F32) for item in out_shape] + [dma(moves), dma(moves)],
-    )(*results)
+        scratch_shapes=[dma(4)],
+    )(*[pltpu.with_memory_space_constraint(item, pltpu.VMEM) for item in results])
 
 
 def solution(mesh):

time: 128 us -> 125 us (0.977)
  Pallas kernels: 126 us -> 123 us
    pallas_call x1, Pallas kernels: 123 us -> 121 us  [body(): pl.pallas_call(functools.partial(kernel, n, g, width, scales), out_shape=...]
where the time goes in v6:
time: 125 us; the launch traced here: 124 us
  Pallas kernels  123 us (98%)
  between operations  1.28 us (1%)
    pallas_call x1, Pallas kernels, body(): pl.pallas_call(functools.partial(kernel, n, g, width, scales), out_shape=...  121 us

profile of v6, /device:TPU:0, one launch (start us, length us, event | category | flops | bytes accessed | tf_op | source)
XLA Modules:
  0.0 124.1 jit_solution(11559856220801728475)
XLA Ops:
  1.3 121.1 %shard_map.84 = (f32[48,128]{1,0:T(8,128)S(1)}, f32[48,16640]{1,0:T(8,128)S(1)}, f32[3,16,16]{2,1,0:T(8,128)S(1)}, f32[3,16,16]{2,1,0:T(8,128)S(1)}) custom-call(s32[1]{0:T(128)S(6)} %copy.9.live, s32[128,16640]{1,0:T(8,128)} %counts.1, f32[32,128]{1,0:T(8,128)} %left_basis.1, f32[32,16640]{1,0:T(8,128)} %right_basis.1, f32[16,16640]{1,0:T(8,128)} %right_start.1), custom_call_target="tpu_custom_call" | custom-call | tf_op jit(solution)/shard_map/pallas_call | solution.py:837
  122.3 1.7 %shard_map.85 = (f32[48,128]{1,0:T(8,128)}, f32[48,16640]{1,0:T(8,128)}, f32[3,16,16]{2,1,0:T(8,128)}, f32[3,16,16]{2,1,0:T(8,128)}) custom-call(f32[48,128]{1,0:T(8,128)S(1)} %get-tuple-element.8.left, f32[48,16640]{1,0:T(8,128)S(1)} %get-tuple-element.9.right, f32[3,16,16]{2,1,0:T(8,128)S(1)} %get-tuple-element.10.diag, ...), custom_call_target="tpu_custom_call" | custom-call | tf_op jit(solution)/shard_map/pallas_call | solution.py:847

commit v7 on v6

--- a/solution.py
+++ b/solution.py
@@ -13,7 +13,7 @@
 STEPS = 3
 SLOTS = BASIS + STEPS * BLOCK
 WEIGHT = SLOTS + BLOCK
-LAG = 2
+LAG = 3
 LANES = 128
 F32 = jnp.float32
 BF16 = jnp.bfloat16
@@ -290,11 +290,12 @@
 
             def one(k):
                 pair(k)
-                join(k - LAG)
-
-            loop(0, LAG, pair)
-            loop(LAG, h, one)
-            loop(h - LAG, h, join)
+                join(k - lag)
+
+            lag = min(LAG, h)
+            loop(0, lag, pair)
+            loop(lag, h, one)
+            loop(h - lag, h, join)
 
         def complete(self, z):
             d = 2 * (z * b + yi) + core
@@ -419,7 +420,7 @@
         both = jnp.concatenate([high, vlo[d, 0 : BASIS + BLOCK]], axis=0)
         xs0[mine] = xs0[mine] + product(high, both, vhi[d], vlo[d], ROWS)
 
-    loop(0, n // 2, meet, 2)
+    loop(0, n // 2, meet, 4)
     gramz[zi] = gathered(along_plane, gram0, seat, 2 * b, g0s_sem, g0r_sem)
     spread(along_column, gramz, zi, a, g0zs_sem, g0zr_sem)
     waited(along_cells, mu, me, n, ms_sem, mr_sem)
@@ -454,14 +455,14 @@
         xb0[mine] = xb0[mine] + met[0:BASIS]
         xg[0, mine] = xg[0, mine] + met[BASIS:]
 
-    loop(0, n // 2, cross, 2)
+    loop(0, n // 2, cross, 4)
     base.third(0, 1)
-    loop(n // 2, n, cross, 2)
+    loop(n // 2, n, cross, 4)
     spread(along_genes, xg.at[0], mine, g, xs_sem.at[0], xr_sem.at[0])
     spread(along_genes, xb0, mine, g, b0s_sem, b0r_sem)
     base.third(1, 2)
 
-    loop(n // 2, n, meet, 2)
+    loop(n // 2, n, meet, 4)
     spread(along_genes, xs0, mine, g, s0s_sem, s0r_sem)
     near = gathered(along_column, gramz, zi, a, g0zs_sem, g0zr_sem)
     corner = lax.broadcasted_iota(jnp.int32, (LANES, LANES), 0)

time: 125 us -> 124 us (level)
  no operation moved by 1% of the time
where the time goes in v7:
time: 124 us
  Pallas kernels  122 us (98%)
  between operations  1.28 us (1%)
    pallas_call x1, Pallas kernels, body(): pl.pallas_call(functools.partial(kernel, n, g, width, scales), out_shape=...  121 us

profile of v7, /device:TPU:0, one launch (start us, length us, event | category | flops | bytes accessed | tf_op | source)
XLA Modules:
  0.0 123.5 jit_solution(10297172389455648453)
XLA Ops:
  1.3 120.5 %shard_map.84 = (f32[48,128]{1,0:T(8,128)S(1)}, f32[48,16640]{1,0:T(8,128)S(1)}, f32[3,16,16]{2,1,0:T(8,128)S(1)}, f32[3,16,16]{2,1,0:T(8,128)S(1)}) custom-call(s32[1]{0:T(128)S(6)} %copy.9.live, s32[128,16640]{1,0:T(8,128)} %counts.1, f32[32,128]{1,0:T(8,128)} %left_basis.1, f32[32,16640]{1,0:T(8,128)} %right_basis.1, f32[16,16640]{1,0:T(8,128)} %right_start.1), custom_call_target="tpu_custom_call" | custom-call | tf_op jit(solution)/shard_map/pallas_call | solution.py:838
  121.8 1.7 %shard_map.85 = (f32[48,128]{1,0:T(8,128)}, f32[48,16640]{1,0:T(8,128)}, f32[3,16,16]{2,1,0:T(8,128)}, f32[3,16,16]{2,1,0:T(8,128)}) custom-call(f32[48,128]{1,0:T(8,128)S(1)} %get-tuple-element.8.left, f32[48,16640]{1,0:T(8,128)S(1)} %get-tuple-element.9.right, f32[3,16,16]{2,1,0:T(8,128)S(1)} %get-tuple-element.10.diag, ...), custom_call_target="tpu_custom_call" | custom-call | tf_op jit(solution)/shard_map/pallas_call | solution.py:848
